TPU v7x, 32 devices: a whole 2x2x4 slice. The times are simulated.
32 devices in a mesh: dp: 8 (over z, y), dap: 4 (over x, core).
Axes of the slice: x: 2, y: 2, z: 4, core: 2. Of those that a mesh axis runs over, the one named last changes fastest.
Arguments:
- single_rep: bfloat16 [8, 128, 384], P('dp', 'dap')
- pair_rep: bfloat16 [8, 128, 128, 128], P('dp', 'dap')
- token_mask: int32 [8, 128], P('dp')
- d_single_out: bfloat16 [8, 128, 384], P('dp', 'dap')
- d_pair_out: bfloat16 [8, 128, 128, 128], P('dp', 'dap')
- mul_out_in: bfloat16 [128, 512], replicated
- mul_out_gate: bfloat16 [128, 128], replicated
- mul_out_proj: bfloat16 [128, 128], replicated
- mul_in_in: bfloat16 [128, 512], replicated
- mul_in_gate: bfloat16 [128, 128], replicated
- mul_in_proj: bfloat16 [128, 128], replicated
- att_st_qkvg: bfloat16 [128, 512], replicated
- att_st_bias: bfloat16 [128, 4], replicated
- att_st_proj: bfloat16 [128, 128], replicated
- att_en_qkvg: bfloat16 [128, 512], replicated
- att_en_bias: bfloat16 [128, 4], replicated
- att_en_proj: bfloat16 [128, 128], replicated
- pair_up: bfloat16 [128, 1024], replicated
- pair_down: bfloat16 [512, 128], replicated
- sing_qkvg: bfloat16 [384, 1536], replicated
- sing_qbias: bfloat16 [384], replicated
- sing_pbias: bfloat16 [128, 16], replicated
- sing_proj: bfloat16 [384, 384], replicated
- sing_up: bfloat16 [384, 3072], replicated
- sing_down: bfloat16 [1536, 384], replicated
Outputs:
- output 1: bfloat16 [8, 128, 384], P('dp', 'dap')
- output 2: bfloat16 [8, 128, 128, 128], P('dp', 'dap')
- output 3: bfloat16 [8, 128, 384], P('dp', 'dap')
- output 4: bfloat16 [8, 128, 128, 128], P('dp', 'dap')
- output 5: float32 [3067264], P('dp')
All inputs are finite; a program needn't handle non-finite values.
Results may differ from a plain program's by a relative error of at most 0.02.
Values are sent between devices in bfloat16 or wider.
A program may use at most 1 GiB of HBM per device.

v0:
```python
import functools
import jax
import jax.numpy as jnp
from jax import lax
from jax.sharding import PartitionSpec as P

BATCH_AXIS = 'dp'
GROUP_AXIS = 'dap'
NORM_EPS = 1e-5
MASK_PENALTY = 1.0e9


def layer_norm(x_in):
    x_f32 = x_in.astype(jnp.float32)
    centered = x_f32 - jnp.mean(x_f32, axis=-1, keepdims=True)
    row_var = jnp.mean(centered * centered, axis=-1, keepdims=True)
    return centered * lax.rsqrt(row_var + NORM_EPS)


def mul_pre(z_rows, w_in, w_gate):
    normed = layer_norm(z_rows).astype(jnp.bfloat16)
    proj_all = jnp.dot(normed, w_in, preferred_element_type=jnp.float32)
    inner_dim = w_in.shape[1] // 4
    left_proj = (jax.nn.sigmoid(proj_all[..., inner_dim:2 * inner_dim]) * proj_all[..., :inner_dim]).astype(jnp.bfloat16)
    right_proj = (jax.nn.sigmoid(proj_all[..., 3 * inner_dim:]) * proj_all[..., 2 * inner_dim:3 * inner_dim]).astype(jnp.bfloat16)
    gate_vals = jax.nn.sigmoid(jnp.dot(normed, w_gate, preferred_element_type=jnp.float32))
    return left_proj, right_proj, gate_vals


def mul_post(z_rows, mixed_sum, gate_vals, w_out):
    normed = layer_norm(mixed_sum).astype(jnp.bfloat16)
    update = gate_vals * jnp.dot(normed, w_out, preferred_element_type=jnp.float32)
    return (z_rows.astype(jnp.float32) + update).astype(jnp.bfloat16)


def att_pre(z_rows, w_qkvg, w_tb):
    normed = layer_norm(z_rows).astype(jnp.bfloat16)
    proj_all = jnp.dot(normed, w_qkvg, preferred_element_type=jnp.float32)
    inner_dim = w_qkvg.shape[1] // 4
    num_heads = w_tb.shape[1]
    head_shape = z_rows.shape[:2] + (num_heads, inner_dim // num_heads)
    q_rows = proj_all[..., :inner_dim].astype(jnp.bfloat16).reshape(head_shape)
    k_rows = proj_all[..., inner_dim:2 * inner_dim].astype(jnp.bfloat16).reshape(head_shape)
    v_rows = proj_all[..., 2 * inner_dim:3 * inner_dim].astype(jnp.bfloat16).reshape(head_shape)
    gate_vals = jax.nn.sigmoid(proj_all[..., 3 * inner_dim:])
    bias_rows = jnp.dot(normed, w_tb, preferred_element_type=jnp.float32).astype(jnp.bfloat16)
    return q_rows, k_rows, v_rows, gate_vals, bias_rows


def att_core(q_rows, k_rows, v_rows, bias_full, mask_bias):
    att_scale = q_rows.shape[-1] ** -0.5
    logits = jnp.einsum('ijhd,ikhd->ihjk', q_rows, k_rows, preferred_element_type=jnp.float32) * att_scale
    logits = logits + jnp.transpose(bias_full, (2, 0, 1)) + mask_bias
    prob_mat = jax.nn.softmax(logits, axis=-1).astype(jnp.bfloat16)
    return jnp.einsum('ihjk,ikhd->ijhd', prob_mat, v_rows, preferred_element_type=jnp.float32)


def gated_out(x_rows, attended, gate_vals, w_o):
    gated = (gate_vals * attended.reshape(gate_vals.shape)).astype(jnp.bfloat16)
    return (x_rows.astype(jnp.float32) + jnp.dot(gated, w_o, preferred_element_type=jnp.float32)).astype(jnp.bfloat16)


def transition(x_rows, w_up, w_down):
    normed = layer_norm(x_rows).astype(jnp.bfloat16)
    hidden = jnp.dot(normed, w_up, preferred_element_type=jnp.float32)
    inner_dim = w_down.shape[0]
    acted = (jax.nn.silu(hidden[..., :inner_dim]) * hidden[..., inner_dim:]).astype(jnp.bfloat16)
    return (x_rows.astype(jnp.float32) + jnp.dot(acted, w_down, preferred_element_type=jnp.float32)).astype(jnp.bfloat16)


def single_pre(s_rows, w_qkvg, q_bias):
    normed = layer_norm(s_rows).astype(jnp.bfloat16)
    proj_all = jnp.dot(normed, w_qkvg, preferred_element_type=jnp.float32)
    inner_dim = w_qkvg.shape[1] // 4
    q_rows = (proj_all[:, :inner_dim] + q_bias.astype(jnp.float32)).astype(jnp.bfloat16)
    k_rows = proj_all[:, inner_dim:2 * inner_dim].astype(jnp.bfloat16)
    v_rows = proj_all[:, 2 * inner_dim:3 * inner_dim].astype(jnp.bfloat16)
    gate_vals = jax.nn.sigmoid(proj_all[:, 3 * inner_dim:])
    return q_rows, k_rows, v_rows, gate_vals


def pair_bias(z_rows, w_pb):
    normed = layer_norm(z_rows).astype(jnp.bfloat16)
    return jnp.dot(normed, w_pb, preferred_element_type=jnp.float32).astype(jnp.bfloat16)


def single_core(q_rows, k_all, v_all, bias_rows, mask_bias):
    num_heads = bias_rows.shape[-1]
    head_dim = q_rows.shape[-1] // num_heads
    q_heads = q_rows.reshape(q_rows.shape[0], num_heads, head_dim)
    k_heads = k_all.reshape(k_all.shape[0], num_heads, head_dim)
    v_heads = v_all.reshape(v_all.shape[0], num_heads, head_dim)
    logits = jnp.einsum('ihd,jhd->hij', q_heads, k_heads, preferred_element_type=jnp.float32) * head_dim ** -0.5
    logits = logits + jnp.transpose(bias_rows, (2, 0, 1)).astype(jnp.float32) + mask_bias
    prob_mat = jax.nn.softmax(logits, axis=-1).astype(jnp.bfloat16)
    return jnp.einsum('hij,jhd->ihd', prob_mat, v_heads, preferred_element_type=jnp.float32)


def gather_rows(x_in):
    return lax.all_gather(x_in, GROUP_AXIS, axis=0, tiled=True)


def scatter_rows(x_in):
    return lax.psum_scatter(x_in, GROUP_AXIS, scatter_dimension=0, tiled=True)


def rows_to_cols(x_in):
    return jnp.transpose(lax.all_to_all(x_in, GROUP_AXIS, 1, 0, tiled=True), (1, 0, 2))


def cols_to_rows(x_in):
    return lax.all_to_all(jnp.transpose(x_in, (1, 0, 2)), GROUP_AXIS, 0, 1, tiled=True)


def mul_out_forward(z_rows, w_in, w_gate, w_out):
    (left_proj, right_proj, gate_vals), pull_pre = jax.vjp(mul_pre, z_rows, w_in, w_gate)
    right_all = gather_rows(right_proj)
    mixed_sum = jnp.einsum('ikc,jkc->ijc', left_proj, right_all, preferred_element_type=jnp.float32)
    z_new, pull_post = jax.vjp(mul_post, z_rows, mixed_sum, gate_vals, w_out)
    return z_new, (pull_pre, pull_post, left_proj, right_all)


def mul_out_backward(dz_new, saved_state):
    pull_pre, pull_post, left_proj, right_all = saved_state
    dz_post, d_mixed, d_gate, g_out = pull_post(dz_new)
    d_mixed = d_mixed.astype(jnp.bfloat16)
    d_left = jnp.einsum('ijc,jkc->ikc', d_mixed, right_all, preferred_element_type=jnp.float32).astype(jnp.bfloat16)
    right_part = jnp.einsum('ijc,ikc->jkc', d_mixed, left_proj, preferred_element_type=jnp.float32)
    d_right = scatter_rows(right_part).astype(jnp.bfloat16)
    dz_pre, g_in, g_gate = pull_pre((d_left, d_right, d_gate))
    return dz_post + dz_pre, [g_in, g_gate, g_out]


def mul_in_forward(z_rows, w_in, w_gate, w_out):
    (left_proj, right_proj, gate_vals), pull_pre = jax.vjp(mul_pre, z_rows, w_in, w_gate)
    left_cols = lax.all_to_all(left_proj, GROUP_AXIS, 1, 0, tiled=True)
    right_all = gather_rows(right_proj)
    mixed_sum = jnp.einsum('kic,kjc->ijc', left_cols, right_all, preferred_element_type=jnp.float32)
    z_new, pull_post = jax.vjp(mul_post, z_rows, mixed_sum, gate_vals, w_out)
    return z_new, (pull_pre, pull_post, left_cols, right_all)


def mul_in_backward(dz_new, saved_state):
    pull_pre, pull_post, left_cols, right_all = saved_state
    dz_post, d_mixed, d_gate, g_out = pull_post(dz_new)
    d_mixed = d_mixed.astype(jnp.bfloat16)
    d_left_cols = jnp.einsum('ijc,kjc->kic', d_mixed, right_all, preferred_element_type=jnp.float32).astype(jnp.bfloat16)
    d_left = lax.all_to_all(d_left_cols, GROUP_AXIS, 0, 1, tiled=True)
    right_part = jnp.einsum('ijc,kic->kjc', d_mixed, left_cols, preferred_element_type=jnp.float32)
    d_right = scatter_rows(right_part).astype(jnp.bfloat16)
    dz_pre, g_in, g_gate = pull_pre((d_left, d_right, d_gate))
    return dz_post + dz_pre, [g_in, g_gate, g_out]


def att_forward(z_rows, mask_bias, w_qkvg, w_tb, w_o):
    (q_rows, k_rows, v_rows, gate_vals, bias_rows), pull_pre = jax.vjp(att_pre, z_rows, w_qkvg, w_tb)
    bias_full = gather_rows(bias_rows).astype(jnp.float32)
    attended, pull_core = jax.vjp(functools.partial(att_core, mask_bias=mask_bias), q_rows, k_rows, v_rows, bias_full)
    z_new, pull_post = jax.vjp(gated_out, z_rows, attended, gate_vals, w_o)
    return z_new, (pull_pre, pull_core, pull_post)


def att_backward(dz_new, saved_state):
    pull_pre, pull_core, pull_post = saved_state
    dz_post, d_att, d_gate, g_out = pull_post(dz_new)
    d_query, d_key, d_value, d_bias_full = pull_core(d_att)
    d_bias = scatter_rows(d_bias_full).astype(jnp.bfloat16)
    dz_pre, g_qkvg, g_bias = pull_pre((d_query, d_key, d_value, d_gate, d_bias))
    return dz_post + dz_pre, [g_qkvg, g_bias, g_out]


def single_forward(s_rows, z_rows, mask_bias, w_qkvg, q_bias, w_pb, w_o, w_up, w_down):
    (q_rows, k_rows, v_rows, gate_vals), pull_pre = jax.vjp(single_pre, s_rows, w_qkvg, q_bias)
    bias_rows, pull_bias = jax.vjp(pair_bias, z_rows, w_pb)
    k_all = gather_rows(k_rows)
    v_all = gather_rows(v_rows)
    attended, pull_core = jax.vjp(functools.partial(single_core, mask_bias=mask_bias), q_rows, k_all, v_all, bias_rows)
    s_mid, pull_post = jax.vjp(gated_out, s_rows, attended, gate_vals, w_o)
    s_new, pull_trans = jax.vjp(transition, s_mid, w_up, w_down)
    return s_new, (pull_pre, pull_bias, pull_core, pull_post, pull_trans)


def single_backward(ds_new, saved_state):
    pull_pre, pull_bias, pull_core, pull_post, pull_trans = saved_state
    ds_mid, g_up, g_down = pull_trans(ds_new)
    ds_post, d_att, d_gate, g_out = pull_post(ds_mid)
    d_query, d_key_all, d_value_all, d_bias_rows = pull_core(d_att)
    d_key = scatter_rows(d_key_all.astype(jnp.float32)).astype(jnp.bfloat16)
    d_value = scatter_rows(d_value_all.astype(jnp.float32)).astype(jnp.bfloat16)
    ds_pre, g_qkvg, g_qbias = pull_pre((d_query, d_key, d_value, d_gate))
    dz_bias, g_pbias = pull_bias(d_bias_rows)
    return ds_post + ds_pre, dz_bias, [g_qkvg, g_qbias, g_pbias, g_out, g_up, g_down]


def device_step(single_blk, pair_blk, mask_blk, d_single_blk, d_pair_blk, *weights):
    s_rows = single_blk[0]
    z_rows = pair_blk[0]
    mask_bias = (mask_blk[0].astype(jnp.float32) - 1.0) * MASK_PENALTY
    z_one, saved_one = mul_out_forward(z_rows, weights[0], weights[1], weights[2])
    z_two, saved_two = mul_in_forward(z_one, weights[3], weights[4], weights[5])
    z_three, saved_three = att_forward(z_two, mask_bias, weights[6], weights[7], weights[8])
    zt_four, saved_four = att_forward(rows_to_cols(z_three), mask_bias, weights[9], weights[10], weights[11])
    z_four = cols_to_rows(zt_four)
    z_five, pull_pair = jax.vjp(transition, z_four, weights[12], weights[13])
    s_out, saved_single = single_forward(s_rows, z_five, mask_bias, *weights[14:20])
    ds_in, dz_bias, single_grads = single_backward(d_single_blk[0], saved_single)
    dz_four, g_pup, g_pdown = pull_pair(d_pair_blk[0] + dz_bias)
    dzt_three, end_grads = att_backward(rows_to_cols(dz_four), saved_four)
    dz_two, start_grads = att_backward(cols_to_rows(dzt_three), saved_three)
    dz_one, in_grads = mul_in_backward(dz_two, saved_two)
    dz_zero, out_grads = mul_out_backward(dz_one, saved_one)
    all_grads = out_grads + in_grads + start_grads + end_grads + [g_pup, g_pdown] + single_grads
    grad_flat = jnp.concatenate([g_item.astype(jnp.float32).reshape(-1) for g_item in all_grads])
    grad_flat = lax.psum(grad_flat, GROUP_AXIS)
    grad_flat = lax.psum_scatter(grad_flat, BATCH_AXIS, scatter_dimension=0, tiled=True)
    return s_out[None], z_five[None], ds_in[None], dz_zero[None], grad_flat


def solution(mesh):
    spec_single = P(BATCH_AXIS, GROUP_AXIS, None)
    spec_pair = P(BATCH_AXIS, GROUP_AXIS, None, None)
    spec_mask = P(BATCH_AXIS, None)

    def block_fn(single_rep, pair_rep, token_mask, d_single_out, d_pair_out, *weights):
        in_specs = (spec_single, spec_pair, spec_mask, spec_single, spec_pair) + tuple(P() for w_item in weights)
        out_specs = (spec_single, spec_pair, spec_single, spec_pair, P(BATCH_AXIS))
        mapped = jax.shard_map(device_step, mesh=mesh, in_specs=in_specs, out_specs=out_specs, check_vma=False)
        return mapped(single_rep, pair_rep, token_mask, d_single_out, d_pair_out, *weights)

    return block_fn
```

profile of v0, /device:TPU:0, one launch (start us, length us, event | category | flops | bytes accessed | tf_op | source)
XLA Modules:
  0.0 1337.5 jit_solution(11685460841675018736)
XLA Ops:
  17.8 37.1 %all-gather.3.cloned.1.call-done = bf16[128,128,128]{2,1,0:T(8,128)(2,1)} async-done(((bf16[32,128,128]{2,1,0:T(8,128)(2,1)}), bf16[128,128,128]{2,1,0:T(8,128)(2,1)}) %all-gather.3.cloned.1.call-update) | async-done | bytes 4194320 | tf_op jit(solution)/shard_map/all_gather | solution.py:100
  54.9 6.7 copy.530
  61.6 4.8 bitcast_reduce_fusion.2
  81.7 3.7 all-to-all-start
  85.4 23.6 %all-to-all-done = bf16[32,128,128]{2,0,1:T(8,128)(2,1)S(1)} async-done(((bf16[32,128,128]{2,0,1:T(8,128)(2,1)}), bf16[32,128,128]{2,0,1:T(8,128)(2,1)S(1)}, u32[]{:S(2)}, u32[]{:S(2)}) %all-to-all-start) | async-done | bytes 1048608 | tf_op jit(solution)/shard_map/all_to_all | solution.py:136
  112.9 10.6 all-gather.5.cloned.1.call-done
  123.5 6.7 copy.545
  130.2 3.4 bitcast_reduce_fusion.1
  141.0 5.4 all_gather.22
  149.0 5.5 fusion.381
  163.4 3.2 slice.116
  169.5 8.2 fusion.382
  177.7 4.9 divide_convert_fusion.1
  192.1 3.5 all-to-all-start.1
  196.6 13.3 all-to-all-done.1
  216.4 5.8 all_gather.23
  224.7 5.5 fusion.383
  237.7 3.6 slice.120
  244.2 8.8 fusion.384
  253.0 4.8 divide_convert_fusion
  265.9 3.6 all-to-all-start.2
  274.0 11.1 all_gather.19
  286.7 5.5 all_gather.18
  308.9 4.0 fusion.233
  312.9 3.2 multiply_convert_fusion
  316.1 3.1 copy-done.14
  340.1 10.9 convert_multiply_fusion.3
  351.0 9.4 fusion.74
  364.0 3.6 all-to-all-start.3
  368.8 13.0 all-to-all-done.3
  389.0 3.3 fusion.391
  392.4 5.4 fusion.7
  397.9 3.4 fusion.120
  406.6 13.8 %all-reduce.33 = bf16[128,128,4]{1,2,0:T(4,128)(2,1)S(1)} all-reduce(f32[128,128,4]{1,2,0:T(4,128)S(1)} %copy.592), channel_id=4, replica_groups=mesh['dp'=8,'dap'=4] {'dap'}, use_global_device_ids=true, to_apply=%region_39.40.clone | all-reduce | flops 65536 | bytes 393216
  420.5 3.9 fusion.116
  433.7 3.5 all-to-all-start.4
  437.3 14.1 %all-to-all-done.4 = bf16[128,32,128]{2,1,0:T(8,128)(2,1)S(1)} async-done(((bf16[128,32,128]{2,1,0:T(8,128)(2,1)}), bf16[128,32,128]{2,1,0:T(8,128)(2,1)S(1)}, u32[]{:S(2)}, u32[]{:S(2)}) %all-to-all-start.4) | async-done | bytes 1048608 | tf_op jit(solution)/shard_map/all_to_all | solution.py:112
  455.3 3.7 fusion.76
  463.5 5.7 fusion.11
  469.3 3.3 fusion.126
  477.9 14.1 %all-reduce.34 = bf16[128,128,4]{1,2,0:T(4,128)(2,1)S(1)} all-reduce(f32[128,128,4]{1,2,0:T(4,128)S(1)} %copy.601), channel_id=5, replica_groups=mesh['dp'=8,'dap'=4] {'dap'}, use_global_device_ids=true, to_apply=%region_44.45.clone | all-reduce | flops 65536 | bytes 393216
  504.1 8.4 copy.761
  512.5 4.5 fusion.144
  519.2 3.6 all-to-all-start.5
  525.5 11.6 all-to-all-done.5
  540.8 43.2 %reduce-scatter.9.cloned.1.call-done = f32[32,128,128]{1,2,0:T(8,128)} async-done(((f32[128,128,128]{1,2,0:T(8,128)}), f32[32,128,128]{1,2,0:T(8,128)}) %reduce-scatter.9.cloned.1.call-update) | async-done | bytes 2097168 | tf_op jit(solution)/shard_map/reduce_scatter | solution.py:104
  584.1 5.1 convert_multiply_fusion.16
  603.4 4.6 fusion.213
  608.0 9.3 copy.622
  631.0 6.8 fusion.148
  652.7 3.6 reshape.535
  659.0 3.5 fusion.163
  667.1 3.5 fusion.164
  676.7 25.2 %reduce-scatter.11.cloned.1.call-done = f32[32,128,128]{1,2,0:T(8,128)} async-done(((f32[128,128,128]{1,2,0:T(8,128)}), f32[32,128,128]{1,2,0:T(8,128)}) %reduce-scatter.11.cloned.1.call-update) | async-done | bytes 2097168 | tf_op jit(solution)/shard_map/reduce_scatter | solution.py:104
  701.9 5.3 convert_multiply_fusion.9
  724.8 3.2 dynamic-update-slice.9
  732.3 4.2 fusion.155
  740.6 5.9 dynamic-update-slice.17
  746.4 36.4 %dynamic-update-slice.18 = bf16[3067264]{0:T(1024)(128)(2,1)} dynamic-update-slice(bf16[3067264]{0:T(1024)(128)(2,1)} %dynamic-update-slice.17, bf16[1179648]{0:T(1024)(128)(2,1)S(1)} %bitcast.638, s32[]{} %constant.160) | dynamic-update-slice | bytes 4718596
  782.9 19.2 %dynamic-update-slice.19 = bf16[3067264]{0:T(1024)(128)(2,1)} dynamic-update-slice(bf16[3067264]{0:T(1024)(128)(2,1)} %dynamic-update-slice.18, bf16[589824]{0:T(1024)(128)(2,1)} %reshape.539, s32[]{} %constant.161) | dynamic-update-slice | bytes 2359300 | tf_op jit(solution)/shard_map/concatenate | solution.py:213
  802.1 479.1 %all-reduce.35 = f32[3067264]{0:T(1024)} all-reduce(bf16[3067264]{0:T(1024)(128)(2,1)} %dynamic-update-slice.19), channel_id=8, replica_groups=mesh['dp'=8,'dap'=4] {'dp'}, use_global_device_ids=true, to_apply=%region_59.60.clone | all-reduce | flops 3067264 | bytes 18403584
  1281.2 3.1 dynamic-slice.5
  1285.0 3.6 fusion.201
  1290.9 36.7 %all-reduce.32.cloned.1.call-done = f32[383408]{0:T(1024)} async-done(((f32[383408]{0:T(1024)}), f32[383408]{0:T(1024)}) %all-reduce.32.cloned.1.call-update) | async-done | bytes 1533648 | tf_op jit(solution)/shard_map/psum | solution.py:214
  (744 shorter events, 278.1 us)
Async XLA Ops:
  7.2 322.1 %copy-start = (bf16[384,3072]{1,0:T(8,128)(2,1)S(1)}, bf16[384,3072]{1,0:T(8,128)(2,1)}, u32[]{:S(2)}) copy-start(bf16[384,3072]{1,0:T(8,128)(2,1)} %param.48) | copy-start | bytes 7077892
  7.2 47.7 %all-gather.3.cloned.1.call-start = ((), (), s32[]{:S(2)}) async-start(), calls=%async_computation.10 | async-start | bytes 5242880 | tf_op jit(solution)/shard_map/all_gather | solution.py:100
  9.0 60.0 %copy-start.15 = (bf16[1,32,128,128]{2,3,1,0:T(8,128)(2,1)}, bf16[1,32,128,128]{2,3,1,0:T(8,128)(2,1)S(1)}, u32[]{:S(2)}) copy-start(bf16[1,32,128,128]{2,3,1,0:T(8,128)(2,1)S(1)} %copy.521) | copy-start | bytes 3145732
  9.2 59.8 %copy-start.112 = (f32[32,128]{1,0:T(8,128)}, f32[32,128]{1,0:T(8,128)S(1)}, u32[]{:S(2)}) copy-start(f32[32,128]{1,0:T(8,128)S(1)} %broadcast_multiply_fusion.7) | copy-start | bytes 49156
  10.2 58.9 %copy-start.128 = (f32[32,128]{1,0:T(8,128)}, f32[32,128]{1,0:T(8,128)S(1)}, u32[]{:S(2)}) copy-start(f32[32,128]{1,0:T(8,128)S(1)} %fusion.308) | copy-start | bytes 49156
  17.7 105.8 %all-gather.5.cloned.1.call-start = ((), (), s32[]{:S(2)}) async-start(), calls=%async_computation.11 | async-start | bytes 5242880 | tf_op jit(solution)/shard_map/all_gather | solution.py:100
  71.8 64.4 %copy-start.114 = (f32[32,128]{1,0:T(8,128)}, f32[32,128]{1,0:T(8,128)S(1)}, u32[]{:S(2)}) copy-start(f32[32,128]{1,0:T(8,128)S(1)} %broadcast_multiply_fusion.5) | copy-start | bytes 49156
  72.7 63.4 %copy-start.131 = (f32[32,128]{1,0:T(8,128)}, f32[32,128]{1,0:T(8,128)S(1)}, u32[]{:S(2)}) copy-start(f32[32,128]{1,0:T(8,128)S(1)} %fusion.310) | copy-start | bytes 49156
  81.7 27.4 %all-to-all-start = ((bf16[32,128,128]{2,0,1:T(8,128)(2,1)}), bf16[32,128,128]{2,0,1:T(8,128)(2,1)S(1)}, u32[]{:S(2)}, u32[]{:S(2)}) async-start(bf16[32,128,128]{2,0,1:T(8,128)(2,1)} %copy.542), calls=%async_computation | async-start | bytes 2097152 | tf_op jit(solution)/shard_map/all_to_all | solution.py:136
  85.4 158.8 %copy-start.224 = (f32[128]{0:T(128)}, f32[128]{0:T(128)S(1)}, u32[]{:S(2)}) copy-start(f32[128]{0:T(128)S(1)} %multiply_bitcast_fusion.1) | copy-start | bytes 1540
  112.9 17.3 %copy-start.60 = (bf16[128,32,128]{0,1,2:T(8,128)(2,1)}, bf16[128,32,128]{0,1,2:T(8,128)(2,1)S(1)}, u32[]{:S(2)}) copy-start(bf16[128,32,128]{0,1,2:T(8,128)(2,1)S(1)} %copy.546) | copy-start | bytes 3145732
  139.7 46.6 %copy-start.38 = (bf16[32,128,128]{1,2,0:T(8,128)(2,1)}, bf16[32,128,128]{1,2,0:T(8,128)(2,1)S(1)}, u32[]{:S(2)}) copy-start(bf16[32,128,128]{1,2,0:T(8,128)(2,1)S(1)} %get-tuple-element.35) | copy-start | bytes 3145732
  139.7 14.8 %copy-start.133 = (f32[32,128]{1,0:T(8,128)}, f32[32,128]{1,0:T(8,128)S(1)}, u32[]{:S(2)}) copy-start(f32[32,128]{1,0:T(8,128)S(1)} %broadcast_multiply_fusion.3) | copy-start | bytes 49156
  140.7 13.8 %copy-start.149 = (f32[32,128]{1,0:T(8,128)}, f32[32,128]{1,0:T(8,128)S(1)}, u32[]{:S(2)}) copy-start(f32[32,128]{1,0:T(8,128)S(1)} %fusion.312) | copy-start | bytes 49156
  189.5 6.8 copy-start.97
  192.1 17.7 %all-to-all-start.1 = ((bf16[32,128,128]{2,0,1:T(8,128)(2,1)}), bf16[32,128,128]{2,0,1:T(8,128)(2,1)S(1)}, u32[]{:S(2)}, u32[]{:S(2)}) async-start(bf16[32,128,128]{2,0,1:T(8,128)(2,1)} %copy.559), calls=%async_computation.1 | async-start | bytes 2097152 | tf_op jit(solution)/shard_map/all_to_all | solution.py:108
  196.4 73.2 %copy-start.210 = (f32[32]{0:T(128)}, f32[32]{0:T(128)S(1)}, u32[]{:S(2)}) copy-start(f32[32]{0:T(128)S(1)} %broadcast_multiply_fusion.9) | copy-start | bytes 388
  196.5 14.0 %copy-start.227 = (f32[32]{0:T(128)}, f32[32]{0:T(128)S(1)}, u32[]{:S(2)}) copy-start(f32[32]{0:T(128)S(1)} %fusion.276) | copy-start | bytes 388
  196.6 73.0 %copy-start.215 = (f32[32]{0:T(128)}, f32[32]{0:T(128)S(1)}, u32[]{:S(2)}) copy-start(f32[32]{0:T(128)S(1)} %fusion.325) | copy-start | bytes 388
  216.0 14.2 %copy-start.51 = (bf16[32,128,128]{2,1,0:T(8,128)(2,1)}, bf16[32,128,128]{2,1,0:T(8,128)(2,1)S(1)}, u32[]{:S(2)}) copy-start(bf16[32,128,128]{2,1,0:T(8,128)(2,1)S(1)} %multiply_convert_fusion.2) | copy-start | bytes 3145732
  237.7 20.1 %copy-start.55 = (bf16[32,128,128]{1,2,0:T(8,128)(2,1)}, bf16[32,128,128]{1,2,0:T(8,128)(2,1)S(1)}, u32[]{:S(2)}) copy-start(bf16[32,128,128]{1,2,0:T(8,128)(2,1)S(1)} %copy.563) | copy-start | bytes 3145732
  265.9 6.6 copy-start.218
  265.9 30.2 %all-to-all-start.2 = ((bf16[128,32,128]{2,1,0:T(8,128)(2,1)}), bf16[128,32,128]{2,1,0:T(8,128)(2,1)S(1)}, u32[]{:S(2)}, u32[]{:S(2)}) async-start(bf16[128,32,128]{2,1,0:T(8,128)(2,1)} %copy.569), calls=%async_computation.2 | async-start | bytes 2097152 | tf_op jit(solution)/shard_map/all_to_all | solution.py:112
  304.0 57.2 %copy-start.135 = (f32[32,128]{1,0:T(8,128)}, f32[32,128]{1,0:T(8,128)S(1)}, u32[]{:S(2)}) copy-start(f32[32,128]{1,0:T(8,128)S(1)} %rsqrt.111) | copy-start | bytes 49156
  312.8 6.3 copy-start.14
  312.9 6.3 copy-start.5
  321.2 17.9 %copy-start.37 = (bf16[32,128,128]{1,2,0:T(8,128)(2,1)}, bf16[32,128,128]{1,2,0:T(8,128)(2,1)S(1)}, u32[]{:S(2)}) copy-start(bf16[32,128,128]{1,2,0:T(8,128)(2,1)S(1)} %get-tuple-element.90) | copy-start | bytes 3145732
  340.1 21.2 %copy-start.83 = (bf16[32,128,128]{1,2,0:T(8,128)(2,1)}, bf16[32,128,128]{1,2,0:T(8,128)(2,1)S(1)}, u32[]{:S(2)}) copy-start(bf16[32,128,128]{1,2,0:T(8,128)(2,1)S(1)} %fusion.196) | copy-start | bytes 3145732
  340.1 10.9 copy-start.6
  340.1 10.9 copy-start.103
  351.0 9.5 copy-start.31
  351.0 9.5 copy-start.182
  362.2 6.5 copy-start.123
  363.9 20.3 %copy-start.49 = (f32[32,128,128]{1,2,0:T(8,128)S(1)}, f32[32,128,128]{1,2,0:T(8,128)}, u32[]{:S(2)}) copy-start(f32[32,128,128]{1,2,0:T(8,128)} %copy.708) | copy-start | bytes 6291460
  364.0 20.3 %copy-start.203 = (bf16[128,128]{1,0:T(8,128)(2,1)S(1)}, bf16[128,128]{1,0:T(8,128)(2,1)}, u32[]{:S(2)}) copy-start(bf16[128,128]{1,0:T(8,128)(2,1)} %param.41) | copy-start | bytes 98308
  364.0 17.8 %all-to-all-start.3 = ((bf16[32,128,128]{2,0,1:T(8,128)(2,1)}), bf16[32,128,128]{2,0,1:T(8,128)(2,1)S(1)}, u32[]{:S(2)}, u32[]{:S(2)}) async-start(bf16[32,128,128]{2,0,1:T(8,128)(2,1)} %copy.589), calls=%async_computation.5 | async-start | bytes 2097152 | tf_op jit(solution)/shard_map/all_to_all | solution.py:108
  384.3 45.1 %copy-start.71 = (bf16[4,32,32,128]{3,1,0,2:T(8,128)(2,1)}, bf16[4,32,32,128]{3,1,0,2:T(8,128)(2,1)S(1)}, u32[]{:S(2)}) copy-start(bf16[4,32,32,128]{3,1,0,2:T(8,128)(2,1)S(1)} %copy.591) | copy-start | bytes 3145732
  389.0 8.8 slice-start.2
  404.1 16.3 %copy-start.185 = (bf16[128,512]{1,0:T(8,128)(2,1)S(1)}, bf16[128,512]{1,0:T(8,128)(2,1)}, u32[]{:S(2)}) copy-start(bf16[128,512]{1,0:T(8,128)(2,1)} %param.39) | copy-start | bytes 393220
  433.7 17.7 %all-to-all-start.4 = ((bf16[128,32,128]{2,1,0:T(8,128)(2,1)}), bf16[128,32,128]{2,1,0:T(8,128)(2,1)S(1)}, u32[]{:S(2)}, u32[]{:S(2)}) async-start(bf16[128,32,128]{2,1,0:T(8,128)(2,1)} %copy.599), calls=%async_computation.6 | async-start | bytes 2097152 | tf_op jit(solution)/shard_map/all_to_all | solution.py:112
  437.3 146.8 %reduce-scatter.9.cloned.1.call-start = ((), (), s32[]{:S(2)}) async-start(), calls=%async_computation.14 | async-start | bytes 10485760 | tf_op jit(solution)/shard_map/reduce_scatter | solution.py:104
  461.2 8.1 slice-start
  463.5 28.6 %copy-start.111 = (bf16[32,4,32,128]{3,2,1,0:T(8,128)(2,1)}, bf16[32,4,32,128]{3,2,1,0:T(8,128)(2,1)S(1)}, u32[]{:S(2)}) copy-start(bf16[32,4,32,128]{3,2,1,0:T(8,128)(2,1)S(1)} %fusion.390) | copy-start | bytes 3145732
  475.5 16.6 %copy-start.186 = (bf16[128,512]{1,0:T(8,128)(2,1)S(1)}, bf16[128,512]{1,0:T(8,128)(2,1)}, u32[]{:S(2)}) copy-start(bf16[128,512]{1,0:T(8,128)(2,1)} %param.36) | copy-start | bytes 393220
  519.2 17.8 %all-to-all-start.5 = ((bf16[128,32,128]{2,1,0:T(8,128)(2,1)}), bf16[128,32,128]{2,1,0:T(8,128)(2,1)S(1)}, u32[]{:S(2)}, u32[]{:S(2)}) async-start(bf16[128,32,128]{2,1,0:T(8,128)(2,1)} %copy.613), calls=%async_computation.8 | async-start | bytes 2097152 | tf_op jit(solution)/shard_map/all_to_all | solution.py:148
  522.9 125.8 %reduce-scatter.7.cloned.1.call-start = ((), (), s32[]{:S(2)}) async-start(), calls=%async_computation.13 | async-start | bytes 245760 | tf_op jit(solution)/shard_map/reduce_scatter | solution.py:104
  524.2 125.3 %reduce-scatter.5.cloned.1.call-start = ((), (), s32[]{:S(2)}) async-start(), calls=%async_computation.12 | async-start | bytes 245760 | tf_op jit(solution)/shard_map/reduce_scatter | solution.py:104
  525.4 176.5 %reduce-scatter.11.cloned.1.call-start = ((), (), s32[]{:S(2)}) async-start(), calls=%async_computation.15 | async-start | bytes 10485760 | tf_op jit(solution)/shard_map/reduce_scatter | solution.py:104
  617.3 7.6 copy-start.158
  617.3 7.6 copy-start.167
  617.4 10.1 copy-start.146
  617.4 710.2 %all-reduce.32.cloned.1.call-start = ((), (), s32[]{:S(2)}) async-start(), calls=%async_computation.16 | async-start | bytes 3072000 | tf_op jit(solution)/shard_map/psum | solution.py:214
  619.2 11.7 copy-start.7
  619.2 11.7 copy-start.136
  647.8 8.4 copy-start.162
  652.7 6.4 copy-start.52
  676.7 30.6 %copy-start.16 = (bf16[1,32,128,128]{2,3,1,0:T(8,128)(2,1)S(1)}, bf16[1,32,128,128]{2,3,1,0:T(8,128)(2,1)}, u32[]{:S(2)}) copy-start(bf16[1,32,128,128]{2,3,1,0:T(8,128)(2,1)} %copy-done.15) | copy-start | bytes 3145732
  676.7 30.6 %copy-start.113 = (f32[32,128]{1,0:T(8,128)S(1)}, f32[32,128]{1,0:T(8,128)}, u32[]{:S(2)}) copy-start(f32[32,128]{1,0:T(8,128)} %copy-done.112) | copy-start | bytes 49156
  676.7 30.6 %copy-start.129 = (f32[32,128]{1,0:T(8,128)S(1)}, f32[32,128]{1,0:T(8,128)}, u32[]{:S(2)}) copy-start(f32[32,128]{1,0:T(8,128)} %copy-done.128) | copy-start | bytes 49156
  719.8 9.5 copy-start.68
  721.1 10.5 copy-start.110
  721.1 11.3 copy-start.84
  736.6 9.9 copy-start.66
  1285.0 45.2 %copy-start.1 = (bf16[384,3072]{1,0:T(8,128)(2,1)S(1)}, bf16[384,3072]{1,0:T(8,128)(2,1)}, u32[]{:S(2)}) copy-start(bf16[384,3072]{1,0:T(8,128)(2,1)} %param.48) | copy-start | bytes 7077892
  (189 other events, 531.3 us)
Sparse Core Ops, SparseCore 0:
  17.8 37.0 all-gather.2
  80.1 43.3 all-gather.4
  512.6 71.4 reduce-scatter.8
  586.9 19.7 reduce-scatter.6
  609.0 19.7 reduce-scatter.4
  631.2 70.6 reduce-scatter.10
  1284.4 43.1 all-reduce.31
where the time goes:
time: 1360 us; the launch traced here: 1340 us
  blocking collectives  535 us (39%)
  local copies, waits for them, and re-layouts  259 us (19%)
  waiting for transfers between devices  229 us (17%)
  matrix products  196 us (14%)
  other arithmetic  79 us (6%)
  starting transfers between devices  22 us (2%)
  between operations  18.9 us (1%)
    unnamed x3, blocking collectives  507 us
    unnamed x509, local copies, waits for them, and re-layouts  122 us
    reduce_scatter x4, waiting for transfers between devices, scatter_rows(): return lax.psum_scatter(x_in, GROUP_AXIS, scatter_dimension=0, tiled=True)  68.5 us
    all_gather x2, waiting for transfers between devices, gather_rows(): return lax.all_gather(x_in, GROUP_AXIS, axis=0, tiled=True)  47.8 us
    psum x1, waiting for transfers between devices, device_step(): grad_flat = lax.psum(grad_flat, GROUP_AXIS)  36.7 us
    all_gather x4, blocking collectives, gather_rows(): return lax.all_gather(x_in, GROUP_AXIS, axis=0, tiled=True)  27.8 us
  transfers between devices with their start and end apart: 13, of which 10 were waited for; matrix products, arithmetic and copies ran while one was open for 9% of the time, Pallas kernels for 0%

commit v1 on v0

v1 whole, which is shorter than its diff:
```python
import functools
import jax
import jax.numpy as jnp
from jax import lax
from jax.experimental import pallas as pl
from jax.experimental.pallas import tpu as pltpu
from jax.sharding import PartitionSpec as P

BATCH_AXIS = 'dp'
GROUP_AXIS = 'dap'
NORM_EPS = 1e-5
MASK_PENALTY = 1.0e9
ROWS_STEP = 4
CHAN_STEP = 8
INTERPRET = False
BF16 = jnp.bfloat16
F32 = jnp.float32


def nn(x, y):
    return lax.dot_general(x, y, (((1,), (0,)), ((), ())), preferred_element_type=F32)


def nt(x, y):
    return lax.dot_general(x, y, (((1,), (1,)), ((), ())), preferred_element_type=F32)


def tn(x, y):
    return lax.dot_general(x, y, (((0,), (0,)), ((), ())), preferred_element_type=F32)


def norm_parts(x):
    xf = x.astype(F32)
    cent = xf - jnp.mean(xf, axis=-1, keepdims=True)
    rstd = lax.rsqrt(jnp.mean(cent * cent, axis=-1, keepdims=True) + NORM_EPS)
    return cent * rstd, rstd


def norm_back(xhat, rstd, dn):
    m1 = jnp.mean(dn, axis=-1, keepdims=True)
    m2 = jnp.mean(dn * xhat, axis=-1, keepdims=True)
    return rstd * (dn - m1 - xhat * m2)


def round_bf(x):
    return x.astype(BF16).astype(F32)


def swap_lead(src, dst):
    steps = src.shape[1] // 16

    def body(t, carry):
        at = pl.ds(pl.multiple_of(t * 16, 16), 16)
        dst[at] = jnp.swapaxes(src[:, at, :], 0, 1)
        return carry
    lax.fori_loop(0, steps, body, 0)


def swap_minor(src, dst, step=4):
    def body(t, carry):
        at = pl.ds(t * step, step)
        dst[at] = jnp.swapaxes(src[at], 1, 2)
        return carry
    lax.fori_loop(0, src.shape[0] // step, body, 0)


def rows_loop(count, body):
    def wrapped(t, carry):
        body(t)
        return carry
    lax.fori_loop(0, count, wrapped, 0)


def call(body, outs, scratch, *args, name):
    outs = [jax.ShapeDtypeStruct(s, d) for s, d in outs]
    return pl.pallas_call(
        body, out_shape=outs, scratch_shapes=scratch, name=name, interpret=INTERPRET,
        in_specs=[pl.BlockSpec(memory_space=pltpu.VMEM)] * len(args),
        out_specs=[pl.BlockSpec(memory_space=pltpu.VMEM)] * len(outs),
        compiler_params=pltpu.CompilerParams(vmem_limit_bytes=56 * 1024 * 1024),
    )(*args)


def mul_pre_body(keep_left, z, w_in, *refs):
    if keep_left:
        left_t, right_t, left_nat, sa, sb = refs
    else:
        left_t, right_t, sa, sb = refs
    width = w_in.shape[1] // 4

    def step(t):
        at = pl.ds(t * ROWS_STEP, ROWS_STEP)
        zc = z[at].reshape(-1, z.shape[-1])
        normed = norm_parts(zc)[0].astype(BF16)
        proj = nn(normed, w_in[...])
        left = (jax.nn.sigmoid(proj[:, width:2 * width]) * proj[:, :width]).astype(BF16)
        right = (jax.nn.sigmoid(proj[:, 3 * width:]) * proj[:, 2 * width:3 * width]).astype(BF16)
        left = left.reshape(ROWS_STEP, -1, width)
        right = right.reshape(ROWS_STEP, -1, width)
        if keep_left:
            left_nat[at] = left
        sa[at] = jnp.swapaxes(left, 1, 2)
        sb[at] = jnp.swapaxes(right, 1, 2)
    rows_loop(z.shape[0] // ROWS_STEP, step)
    swap_lead(sa, left_t)
    swap_lead(sb, right_t)


def mul_pre(z, w_in, keep_left):
    r, n, c = z.shape
    width = w_in.shape[1] // 4
    outs = [((width, r, n), BF16)] * 2 + ([((r, n, width), BF16)] if keep_left else [])
    scratch = [pltpu.VMEM((r, width, n), BF16)] * 2
    return call(functools.partial(mul_pre_body, keep_left), outs, scratch, z, w_in,
                name='mul_pre_in' if keep_left else 'mul_pre_out')


def joined(ref, ch):
    return jnp.concatenate([ref[dev, ch] for dev in range(ref.shape[0])], axis=0)


def mul_post_body(incoming, left, right_g, z, w_gate, w_out, w_tb, z_new, xh_nat, xhat, rstd, bias, *scr):
    tb, t2 = scr[0], scr[1]
    width = xhat.shape[0]
    if incoming:
        u1, u2, u3 = scr[2], scr[3], scr[4]
        swap_lead(left, u1)
        swap_minor(u1, u2)
        swap_lead(u2, u3)
        left = u3

    def mix(t):
        for s in range(CHAN_STEP):
            ch = t * CHAN_STEP + s
            if incoming:
                xhat[ch] = nn(left[ch], joined(right_g, ch))
            else:
                xhat[ch] = nt(left[ch], joined(right_g, ch))
    rows_loop(width // CHAN_STEP, mix)
    zero = jnp.zeros(xhat.shape[1:], F32)
    total = lax.fori_loop(0, width, lambda ch, acc: acc + xhat[ch], zero)
    mean = total / width
    sq = lax.fori_loop(0, width, lambda ch, acc: acc + (xhat[ch] - mean) * (xhat[ch] - mean), zero)
    inv = lax.rsqrt(sq / width + NORM_EPS)
    rstd[...] = inv

    def scale(ch):
        val = (xhat[ch] - mean) * inv
        xhat[ch] = val
        tb[ch] = val.astype(BF16)
    rows_loop(width, scale)
    swap_lead(tb, t2)

    def step(t):
        at = pl.ds(t * ROWS_STEP, ROWS_STEP)
        zc = z[at].reshape(-1, z.shape[-1])
        xh = jnp.swapaxes(t2[at], 1, 2)
        xh_nat[at] = xh
        normed = norm_parts(zc)[0].astype(BF16)
        gate = jax.nn.sigmoid(nn(normed, w_gate[...]))
        upd = gate * nn(xh.reshape(-1, width), w_out[...])
        znew = (zc.astype(F32) + upd).astype(BF16)
        z_new[at] = znew.reshape(ROWS_STEP, -1, z.shape[-1])
        if incoming:
            bias_rows(znew, w_tb, bias, t)
    rows_loop(z.shape[0] // ROWS_STEP, step)
    if not incoming:
        bias[...] = jnp.zeros_like(bias)


def bias_rows(zc, w_t, bias, t):
    normed = norm_parts(zc)[0].astype(BF16).reshape(ROWS_STEP, -1, zc.shape[-1])
    for s in range(ROWS_STEP):
        bias[t * ROWS_STEP + s] = nt(w_t[...], normed[s]).astype(BF16)


def mul_post(left, right_g, z, w_gate, w_out, w_tb, incoming):
    r, n, c = z.shape
    width = w_out.shape[0]
    outs = [((r, n, c), BF16), ((r, n, width), BF16), ((width, r, n), F32), ((r, n), F32), ((r, 16, n), BF16)]
    scratch = [pltpu.VMEM((width, r, n), BF16), pltpu.VMEM((r, width, n), BF16)]
    if incoming:
        scratch += [pltpu.VMEM((r, n, width), BF16), pltpu.VMEM((r, width, n), BF16), pltpu.VMEM((width, r, n), BF16)]
    return call(functools.partial(mul_post_body, incoming), outs, scratch, left, right_g, z, w_gate, w_out, w_tb,
                name='mul_post_in' if incoming else 'mul_post_out')


def mul_back_post_body(want_nat, dz, z, xh_nat, xhat, rstd, w_gate, w_out, d_t, dgp, g_out, *refs):
    if want_nat:
        d_nat, td, td2 = refs
    else:
        td, td2 = refs
    width = xhat.shape[0]
    g_out[...] = jnp.zeros_like(g_out)

    def step(t):
        at = pl.ds(t * ROWS_STEP, ROWS_STEP)
        zc = z[at].reshape(-1, z.shape[-1])
        dzf = dz[at].reshape(-1, z.shape[-1]).astype(F32)
        xh = xh_nat[at].reshape(-1, width)
        normed = norm_parts(zc)[0].astype(BF16)
        gate = jax.nn.sigmoid(nn(normed, w_gate[...]))
        y = nn(xh, w_out[...])
        dgp[at] = (dzf * y * gate * (1.0 - gate)).astype(BF16).reshape(ROWS_STEP, -1, z.shape[-1])
        dy = (dzf * gate).astype(BF16)
        g_out[...] += tn(xh, dy)
        dxh = nt(dy, w_out[...]).astype(BF16).reshape(ROWS_STEP, -1, width)
        td[at] = jnp.swapaxes(dxh, 1, 2)
    rows_loop(z.shape[0] // ROWS_STEP, step)
    swap_lead(td, td2)
    zero = jnp.zeros(xhat.shape[1:], F32)

    def sums(ch, acc):
        d = td2[ch].astype(F32)
        return acc[0] + d, acc[1] + d * xhat[ch]
    s1, s2 = lax.fori_loop(0, width, sums, (zero, zero))
    s1, s2, inv = s1 / width, s2 / width, rstd[...]

    def fin(ch):
        d_t[ch] = (inv * (td2[ch].astype(F32) - s1 - xhat[ch] * s2)).astype(BF16)
    rows_loop(width, fin)
    if want_nat:
        swap_lead(d_t, td)
        swap_minor(td, d_nat)


def mul_back_post(dz, z, xh_nat, xhat, rstd, w_gate, w_out, want_nat):
    r, n, c = z.shape
    width = w_out.shape[0]
    outs = [((width, r, n), BF16), ((r, n, c), BF16), ((width, c), F32)]
    if want_nat:
        outs.append(((r, n, width), BF16))
    scratch = [pltpu.VMEM((r, width, n), BF16), pltpu.VMEM((width, r, n), BF16)]
    return call(functools.partial(mul_back_post_body, want_nat), outs, scratch, dz, z, xh_nat, xhat, rstd, w_gate, w_out,
                name='mul_back_post')


def mul_back_pre_body(incoming, dz, z, dgp, opa, opb, opc, opd, w_in, w_gate, dz_in, g_in, g_gate, da_t, db_t, da_r, db_r,
                      *scr):
    width = w_in.shape[1] // 4
    if incoming:
        d_g, left_t, right_t = opa, opb, opc
    else:
        d_t, d_recv, right_g, left_g = opa, opb, opc, opd
        u1, u2, u3 = scr
        swap_lead(d_recv, u1)
        swap_minor(u1, u2)
        swap_lead(u2, u3)

    def mix(t):
        for s in range(CHAN_STEP):
            ch = t * CHAN_STEP + s
            if incoming:
                d_all = joined(d_g, ch)
                da_t[ch] = nt(right_t[ch], d_all).astype(BF16)
                db_t[ch] = nn(left_t[ch], d_all).astype(BF16)
            else:
                da_t[ch] = nn(d_t[ch], joined(right_g, ch)).astype(BF16)
                db_t[ch] = nn(u3[ch], joined(left_g, ch)).astype(BF16)
    rows_loop(width // CHAN_STEP, mix)
    swap_lead(da_t, da_r)
    swap_lead(db_t, db_r)
    g_in[...] = jnp.zeros_like(g_in)
    g_gate[...] = jnp.zeros_like(g_gate)

    def step(t):
        at = pl.ds(t * ROWS_STEP, ROWS_STEP)
        c = z.shape[-1]
        zc = z[at].reshape(-1, c)
        da = jnp.swapaxes(da_r[at], 1, 2).reshape(-1, width).astype(F32)
        db = jnp.swapaxes(db_r[at], 1, 2).reshape(-1, width).astype(F32)
        zhat, inv = norm_parts(zc)
        normed = zhat.astype(BF16)
        proj = nn(normed, w_in[...])
        sa = jax.nn.sigmoid(proj[:, width:2 * width])
        sb = jax.nn.sigmoid(proj[:, 3 * width:])
        dproj = jnp.concatenate([
            (da * sa).astype(BF16), (da * proj[:, :width] * sa * (1.0 - sa)).astype(BF16),
            (db * sb).astype(BF16), (db * proj[:, 2 * width:3 * width] * sb * (1.0 - sb)).astype(BF16)], axis=1)
        dg = dgp[at].reshape(-1, c)
        g_in[...] += tn(normed, dproj)
        g_gate[...] += tn(normed, dg)
        dn = round_bf(nt(dproj, w_in[...]) + nt(dg, w_gate[...]))
        out = dz[at].reshape(-1, c).astype(F32) + norm_back(zhat, inv, dn)
        dz_in[at] = out.astype(BF16).reshape(ROWS_STEP, -1, c)
    rows_loop(z.shape[0] // ROWS_STEP, step)


def mul_back_pre(dz, z, dgp, opa, opb, opc, opd, w_in, w_gate, incoming):
    r, n, c = z.shape
    width = w_in.shape[1] // 4
    outs = [((r, n, c), BF16), (w_in.shape, F32), (w_gate.shape, F32)]
    scratch = [pltpu.VMEM((width, r, n), BF16)] * 2 + [pltpu.VMEM((r, width, n), BF16)] * 2
    if not incoming:
        scratch += [pltpu.VMEM((r, n, width), BF16), pltpu.VMEM((r, width, n), BF16), pltpu.VMEM((width, r, n), BF16)]
    return call(functools.partial(mul_back_pre_body, incoming), outs, scratch, dz, z, dgp, opa, opb, opc, opd, w_in, w_gate,
                name='mul_back_pre_in' if incoming else 'mul_back_pre_out')


def head_masks(width, heads):
    lane = lax.broadcasted_iota(jnp.int32, (1, width), 1)
    size = width // heads
    return [(lane >= h * size) & (lane < (h + 1) * size) for h in range(heads)]


def stack_heads(x, masks):
    zero = jnp.zeros_like(x)
    return jnp.concatenate([jnp.where(m, x, zero) for m in masks], axis=0)


def pick_heads(x, masks):
    n = x.shape[0] // len(masks)
    out = x[:n]
    for h in range(1, len(masks)):
        out = jnp.where(masks[h], x[h * n:(h + 1) * n], out)
    return out


def load_bias(bias_g, bias_s, add_mask, heads):
    n = bias_g.shape[0]
    for h in range(heads):
        bias_s[h * n:(h + 1) * n] = bias_g[:, h, :].astype(F32) + add_mask


def soft(logits):
    top = jnp.max(logits, axis=-1, keepdims=True)
    e = jnp.exp(logits - top)
    return e / jnp.sum(e, axis=-1, keepdims=True)


def att_body(heads, z, bias_g, mask, w_qkvg, w_o, z_new, bias_s):
    width = w_o.shape[0]
    n = z.shape[1]
    masks = head_masks(width, heads)
    scale = (width // heads) ** -0.5
    load_bias(bias_g, bias_s, mask[...], heads)

    def step(t):
        at = pl.ds(t * ROWS_STEP, ROWS_STEP)
        zc = z[at].reshape(-1, z.shape[-1])
        normed = norm_parts(zc)[0].astype(BF16)
        proj = nn(normed, w_qkvg[...])
        qkv = proj[:, :3 * width].astype(BF16)
        outs = []
        for s in range(ROWS_STEP):
            row = qkv[s * n:(s + 1) * n]
            q, k, v = row[:, :width], row[:, width:2 * width], row[:, 2 * width:]
            prob = soft(nt(stack_heads(q, masks), k) * scale + bias_s[...]).astype(BF16)
            outs.append(pick_heads(nn(prob, v), masks))
        att = jnp.concatenate(outs, axis=0)
        gated = (jax.nn.sigmoid(proj[:, 3 * width:]) * att).astype(BF16)
        out = (zc.astype(F32) + nn(gated, w_o[...])).astype(BF16)
        z_new[at] = out.reshape(ROWS_STEP, n, -1)
    rows_loop(z.shape[0] // ROWS_STEP, step)


def att_fwd(z, bias_g, mask, w_qkvg, w_o, heads):
    n = z.shape[1]
    return call(functools.partial(att_body, heads), [(z.shape, BF16)], [pltpu.VMEM((heads * n, n), F32)],
                z, bias_g, mask, w_qkvg, w_o, name='att_fwd')[0]


def att_back_body(heads, dz, z, bias_g, mask, w_qkvg, w_o, dz_part, d_bias, g_qkvg, g_o, bias_s):
    width = w_o.shape[0]
    n, c = z.shape[1:]
    masks = head_masks(width, heads)
    scale = (width // heads) ** -0.5
    load_bias(bias_g, bias_s, mask[...], heads)
    d_bias[...] = jnp.zeros_like(d_bias)
    g_qkvg[...] = jnp.zeros_like(g_qkvg)
    g_o[...] = jnp.zeros_like(g_o)
    step_rows = 2

    def step(t):
        at = pl.ds(t * step_rows, step_rows)
        zc = z[at].reshape(-1, c)
        dzc = dz[at].reshape(-1, c)
        zhat, inv = norm_parts(zc)
        normed = zhat.astype(BF16)
        proj = nn(normed, w_qkvg[...])
        qkv = proj[:, :3 * width].astype(BF16)
        gate = jax.nn.sigmoid(proj[:, 3 * width:])
        d_gated = round_bf(nt(dzc, w_o[...]))
        d_att = (d_gated * gate).astype(BF16)
        atts, dprojs = [], []
        for s in range(step_rows):
            row = qkv[s * n:(s + 1) * n]
            q, k, v = row[:, :width], row[:, width:2 * width], row[:, 2 * width:]
            qs = stack_heads(q, masks)
            prob = soft(nt(qs, k) * scale + bias_s[...])
            prob_b = prob.astype(BF16)
            att = pick_heads(nn(prob_b, v), masks)
            das = stack_heads(d_att[s * n:(s + 1) * n], masks)
            dp = round_bf(nt(das, v))
            ds = prob * (dp - jnp.sum(prob * dp, axis=-1, keepdims=True))
            d_bias[...] += ds
            dsb = (ds * scale).astype(BF16)
            dq = pick_heads(nn(dsb, k), masks)
            dk = tn(dsb, qs)
            dv = tn(prob_b, das)
            atts.append(att)
            dprojs.append(jnp.concatenate([dq.astype(BF16), dk.astype(BF16), dv.astype(BF16)], axis=1))
        att = jnp.concatenate(atts, axis=0)
        d_gl = (d_gated * att * gate * (1.0 - gate)).astype(BF16)
        gated = (gate * att).astype(BF16)
        dproj = jnp.concatenate([jnp.concatenate(dprojs, axis=0), d_gl], axis=1)
        g_o[...] += tn(gated, dzc)
        g_qkvg[...] += tn(normed, dproj)
        dn = round_bf(nt(dproj, w_qkvg[...]))
        out = dzc.astype(F32) + norm_back(zhat, inv, dn)
        dz_part[at] = out.reshape(step_rows, n, c)
    rows_loop(z.shape[0] // step_rows, step)


def att_back(dz, z, bias_g, mask, w_qkvg, w_o, heads):
    n = z.shape[1]
    outs = [(z.shape, F32), ((heads * n, n), F32), (w_qkvg.shape, F32), (w_o.shape, F32)]
    return call(functools.partial(att_back_body, heads), outs, [pltpu.VMEM((heads * n, n), F32)],
                dz, z, bias_g, mask, w_qkvg, w_o, name='att_back')


def bias_back_rows(zc, db, w_t, g_t, t):
    zhat, inv = norm_parts(zc)
    normed = zhat.astype(BF16).reshape(ROWS_STEP, -1, zc.shape[-1])
    dns = []
    for s in range(ROWS_STEP):
        d = db[t * ROWS_STEP + s]
        dns.append(tn(d, w_t[...]))
        g_t[...] += nn(d, normed[s])
    return norm_back(zhat, inv, round_bf(jnp.concatenate(dns, axis=0)))


def bias_back_body(swap_out, dz_part, z, db, w_t, dz, g_t, *scr):
    g_t[...] = jnp.zeros_like(g_t)
    dst = scr[0] if swap_out else dz

    def step(t):
        at = pl.ds(t * ROWS_STEP, ROWS_STEP)
        c = z.shape[-1]
        add = bias_back_rows(z[at].reshape(-1, c), db, w_t, g_t, t)
        dst[at] = (dz_part[at].reshape(-1, c) + add).astype(BF16).reshape(ROWS_STEP, -1, c)
    rows_loop(z.shape[0] // ROWS_STEP, step)
    if swap_out:
        swap_lead(scr[0], dz)


def bias_back(dz_part, z, db, w_t, swap_out):
    r, n, c = z.shape
    out = (n, r, c) if swap_out else (r, n, c)
    scratch = [pltpu.VMEM((r, n, c), BF16)] if swap_out else []
    return call(functools.partial(bias_back_body, swap_out), [(out, BF16), (w_t.shape, F32)], scratch,
                dz_part, z, db, w_t, name='bias_back')


def turn_body(recv, w_t, z_cols, bias):
    swap_lead(recv, z_cols)

    def step(t):
        zc = z_cols[pl.ds(t * ROWS_STEP, ROWS_STEP)].reshape(-1, z_cols.shape[-1])
        bias_rows(zc, w_t, bias, t)
    rows_loop(z_cols.shape[0] // ROWS_STEP, step)


def turn(recv, w_t):
    n, r, c = recv.shape
    return call(turn_body, [((r, n, c), BF16), ((r, 16, n), BF16)], [], recv, w_t, name='turn')


def pair_trans_body(z, w_up, w_down, w_t, z_new, z_turn, bias):
    inner = w_down.shape[0]

    def step(t):
        at = pl.ds(t * ROWS_STEP, ROWS_STEP)
        zc = z[at].reshape(-1, z.shape[-1])
        normed = norm_parts(zc)[0].astype(BF16)
        hid = nn(normed, w_up[...])
        acted = (jax.nn.silu(hid[:, :inner]) * hid[:, inner:]).astype(BF16)
        out = (zc.astype(F32) + nn(acted, w_down[...])).astype(BF16)
        z_new[at] = out.reshape(ROWS_STEP, -1, z.shape[-1])
        bias_rows(out, w_t, bias, t)
    rows_loop(z.shape[0] // ROWS_STEP, step)
    swap_lead(z_new, z_turn)


def pair_trans(z, w_up, w_down, w_t):
    r, n, c = z.shape
    return call(pair_trans_body, [((r, n, c), BF16), ((n, r, c), BF16), ((r, 16, n), BF16)], [],
                z, w_up, w_down, w_t, name='pair_trans')


def silu_parts(h1, h2):
    sg = jax.nn.sigmoid(h1)
    return sg, h1 * sg


def pair_trans_back_body(d_recv, z5, db, z, w_up, w_down, w_t, dz_in, g_up, g_down, g_t, dz5):
    inner = w_down.shape[0]
    g_up[...] = jnp.zeros_like(g_up)
    g_down[...] = jnp.zeros_like(g_down)
    g_t[...] = jnp.zeros_like(g_t)
    swap_lead(d_recv, dz5)

    def step(t):
        at = pl.ds(t * ROWS_STEP, ROWS_STEP)
        c = z.shape[-1]
        add = bias_back_rows(z5[at].reshape(-1, c), db, w_t, g_t, t)
        dzc = (dz5[at].reshape(-1, c).astype(F32) + add).astype(BF16)
        zhat, inv = norm_parts(z[at].reshape(-1, c))
        normed = zhat.astype(BF16)
        hid = nn(normed, w_up[...])
        h1, h2 = hid[:, :inner], hid[:, inner:]
        sg, si = silu_parts(h1, h2)
        acted = (si * h2).astype(BF16)
        d_act = round_bf(nt(dzc, w_down[...]))
        d1 = (d_act * h2 * (sg + si * (1.0 - sg))).astype(BF16)
        d2 = (d_act * si).astype(BF16)
        dh = jnp.concatenate([d1, d2], axis=1)
        g_down[...] += tn(acted, dzc)
        g_up[...] += tn(normed, dh)
        dn = round_bf(nt(dh, w_up[...]))
        out = dzc.astype(F32) + norm_back(zhat, inv, dn)
        dz_in[at] = out.astype(BF16).reshape(ROWS_STEP, -1, c)
    rows_loop(z.shape[0] // ROWS_STEP, step)


def pair_trans_back(d_recv, z5, db, z, w_up, w_down, w_t):
    r, n, c = z.shape
    outs = [((r, n, c), BF16), (w_up.shape, F32), (w_down.shape, F32), (w_t.shape, F32)]
    return call(pair_trans_back_body, outs, [pltpu.VMEM((r, n, c), BF16)], d_recv, z5, db, z, w_up, w_down, w_t,
                name='pair_trans_back')


def put_rows(out, first, blocks, block, value):
    out[pl.ds(first + block, value.shape[0], stride=blocks), :] = value


def single_body(heads, s, ds, pb_g, mask_col, w_qkvg, q_bias, w_o, w_up, w_down, s_new, ds_in, d_pb, grads,
                pb_t, probs, acc_a, acc_b, acc_c, dh_s, act_s):
    c = s.shape[1]
    n = s.shape[0]
    inner = w_down.shape[0]
    size = c // heads
    scale = size ** -0.5
    lane = lax.broadcasted_iota(jnp.int32, (1, c), 1)
    swap_lead(pb_g, pb_t)

    def masked(x, h):
        return jnp.where((lane >= h * size) & (lane < (h + 1) * size), x, jnp.zeros_like(x))

    s_hat, s_inv = norm_parts(s[...])
    normed = s_hat.astype(BF16)
    proj = nn(normed, w_qkvg[...])
    q = (proj[:, :c] + q_bias[...].astype(F32)).astype(BF16)
    k = proj[:, c:2 * c].astype(BF16)
    v = proj[:, 2 * c:3 * c].astype(BF16)
    gate = jax.nn.sigmoid(proj[:, 3 * c:])
    acc_a[...] = jnp.zeros_like(acc_a)

    def attend(h):
        logits = nt(k, masked(q, h)) * scale + pb_t[h].astype(F32) + mask_col[...]
        e = jnp.exp(logits - jnp.max(logits, axis=0, keepdims=True))
        prob = e / jnp.sum(e, axis=0, keepdims=True)
        probs[h] = prob
        acc_a[...] += tn(prob.astype(BF16), masked(v, h))
    rows_loop(heads, attend)
    att = acc_a[...]
    gated = (gate * att).astype(BF16)
    s_mid = (s[...].astype(F32) + nn(gated, w_o[...])).astype(BF16)
    m_hat, m_inv = norm_parts(s_mid)
    mid_n = m_hat.astype(BF16)
    width = c
    dsv = ds[...]
    acc_b[...] = jnp.zeros_like(acc_b)
    acc_c[...] = jnp.zeros_like(acc_c)
    for t in range(inner // width):
        at = slice(t * width, (t + 1) * width)
        at2 = slice(inner + t * width, inner + (t + 1) * width)
        h1 = nn(mid_n, w_up[:, at])
        h2 = nn(mid_n, w_up[:, at2])
        sg, si = silu_parts(h1, h2)
        act = (si * h2).astype(BF16)
        acc_b[...] += nn(act, w_down[at, :])
        act_s[:, at] = act
        d_act = round_bf(nt(dsv, w_down[at, :]))
        d1 = (d_act * h2 * (sg + si * (1.0 - sg))).astype(BF16)
        d2 = (d_act * si).astype(BF16)
        dh_s[:, at] = d1
        dh_s[:, at2] = d2
        acc_c[...] += nt(d1, w_up[:, at]) + nt(d2, w_up[:, at2])
    s_new[...] = (s_mid.astype(F32) + acc_b[...]).astype(BF16)
    ds_mid = (dsv.astype(F32) + norm_back(m_hat, m_inv, round_bf(acc_c[...]))).astype(BF16)
    rows_qkvg = c * 4 * c // 128
    off_o = rows_qkvg + c // 128 + pb_t.shape[0]
    off_up = off_o + c * c // 128
    off_down = off_up + c * 2 * inner // 128
    cb = c // 128
    for t in range(2 * inner // c):
        g = tn(mid_n, dh_s[:, t * c:(t + 1) * c])
        for b in range(cb):
            put_rows(grads, off_up, 2 * inner // 128, t * cb + b, g[:, b * 128:(b + 1) * 128])
    for t in range(inner // c):
        g = tn(act_s[:, t * c:(t + 1) * c], dsv)
        for b in range(cb):
            put_rows(grads, off_down + t * c * cb, cb, b, g[:, b * 128:(b + 1) * 128])
    g = tn(gated, ds_mid)
    for b in range(cb):
        put_rows(grads, off_o, cb, b, g[:, b * 128:(b + 1) * 128])

    d_gated = round_bf(nt(ds_mid, w_o[...]))
    d_att = (d_gated * gate).astype(BF16)
    d_gl = (d_gated * att * gate * (1.0 - gate)).astype(BF16)
    acc_a[...] = jnp.zeros_like(acc_a)
    acc_b[...] = jnp.zeros_like(acc_b)
    acc_c[...] = jnp.zeros_like(acc_c)

    def back(h):
        prob = probs[h]
        dam = masked(d_att, h)
        dp = round_bf(nt(v, dam))
        dst = prob * (dp - jnp.sum(prob * dp, axis=0, keepdims=True))
        d_pb[h] = dst.astype(BF16)
        dsb = (dst * scale).astype(BF16)
        acc_a[...] += tn(dsb, masked(k, h))
        acc_b[...] += nn(dsb, masked(q, h))
        acc_c[...] += nn(prob.astype(BF16), dam)
    rows_loop(heads, back)
    parts = [acc_a[...].astype(BF16), acc_b[...].astype(BF16), acc_c[...].astype(BF16), d_gl]
    dn = jnp.zeros((n, c), F32)
    for t in range(4):
        g = tn(normed, parts[t])
        dn = dn + nt(parts[t], w_qkvg[:, t * c:(t + 1) * c])
        for b in range(cb):
            put_rows(grads, 0, 4 * cb, t * cb + b, g[:, b * 128:(b + 1) * 128])
    qb = jnp.sum(parts[0].astype(F32), axis=0, keepdims=True)
    for b in range(cb):
        grads[rows_qkvg + b:rows_qkvg + b + 1, :] = qb[:, b * 128:(b + 1) * 128]
    grads[rows_qkvg + cb:off_o, :] = jnp.zeros((off_o - rows_qkvg - cb, 128), F32)
    ds_in[...] = (ds_mid.astype(F32) + norm_back(s_hat, s_inv, round_bf(dn))).astype(BF16)


def single_track(s, ds, pb_g, mask_col, w_qkvg, q_bias, w_o, w_up, w_down, heads):
    n, c = s.shape
    inner = w_down.shape[0]
    rows = (4 * c * c + c + 128 * heads + c * c + 3 * inner * c) // 128
    outs = [((n, c), BF16), ((n, c), BF16), ((heads, n, n), BF16), ((rows, 128), F32)]
    scratch = [pltpu.VMEM((heads, n, n), BF16), pltpu.VMEM((heads, n, n), F32)] + [pltpu.VMEM((n, c), F32)] * 3 + [
        pltpu.VMEM((n, 2 * inner), BF16), pltpu.VMEM((n, inner), BF16)]
    return call(functools.partial(single_body, heads), outs, scratch, s, ds, pb_g, mask_col, w_qkvg, q_bias, w_o, w_up,
                w_down, name='single_track')


def gather(x):
    return lax.all_gather(x, GROUP_AXIS, axis=0, tiled=False)


def gather_rows(x):
    return lax.all_gather(x, GROUP_AXIS, axis=0, tiled=True)


def exchange(x):
    return lax.all_to_all(x, GROUP_AXIS, 1, 0, tiled=True)


def exchange_back(x):
    return lax.all_to_all(x, GROUP_AXIS, 0, 1, tiled=True)


def reduce_bias(d_bias, heads, group):
    n = d_bias.shape[1]
    parts = d_bias.reshape(heads, group, n // group, n).transpose(1, 0, 2, 3)
    own = lax.psum_scatter(parts, GROUP_AXIS, scatter_dimension=0, tiled=False)
    own = own.astype(BF16).transpose(1, 0, 2)
    return jnp.pad(own, ((0, 0), (0, 16 - heads), (0, 0)))


def pad_bias(w_tb):
    return jnp.pad(w_tb.T, ((0, 16 - w_tb.shape[1]), (0, 0)))


def bias_grad(g_t, heads):
    return g_t[:heads].T.reshape(-1, 128)


def chunk_rows(total, parts):
    shard = total // parts
    return shard, -(-(shard // 128 + 2) // 32) * 32


def reduce_single(grads, n_pair, total):
    parts, group = lax.axis_size(BATCH_AXIS), lax.axis_size(GROUP_AXIS)
    shard, chunk = chunk_rows(total, parts)
    quarter = chunk // group
    q = lax.axis_index(GROUP_AXIS)
    padded = jnp.pad(grads, ((n_pair, chunk), (0, 0)))
    pieces = [lax.dynamic_slice(padded, (d * shard // 128 + q * quarter, 0), (quarter, 128)) for d in range(parts)]
    own = lax.psum_scatter(jnp.concatenate(pieces), BATCH_AXIS, scatter_dimension=0, tiled=True)
    return gather_rows(own)


def finish_grads(own, pair_rows, g_pb, pb_row, total):
    parts, group = lax.axis_size(BATCH_AXIS), lax.axis_size(GROUP_AXIS)
    shard, chunk = chunk_rows(total, parts)
    n_pair, n_pb = pair_rows.shape[0], g_pb.shape[0]
    rows = jnp.concatenate([pair_rows, g_pb])
    rows = jnp.pad(rows, ((0, -rows.shape[0] % (8 * group)), (0, 0)))
    rows = lax.psum_scatter(rows, GROUP_AXIS, scatter_dimension=0, tiled=True)
    rows = gather_rows(lax.psum(rows, BATCH_AXIS))
    first = lax.axis_index(BATCH_AXIS) * shard // 128
    pair = jnp.pad(rows[:n_pair], ((0, 2 * chunk), (0, 0)))
    own = own + lax.dynamic_slice(pair, (jnp.minimum(first, n_pair + chunk), 0), (chunk, 128))
    extra = jnp.pad(rows[n_pair:n_pair + n_pb], ((chunk, chunk), (0, 0)))
    at = jnp.clip(chunk - (pb_row - first), 0, chunk + n_pb)
    own = own + lax.dynamic_slice(extra, (at, 0), (chunk, 128))
    offset = (lax.axis_index(BATCH_AXIS) * shard) % 128
    return lax.dynamic_slice(own.reshape(-1), (offset,), (shard,))


def device_step(single_blk, pair_blk, mask_blk, d_single_blk, d_pair_blk, *weights):
    group = lax.axis_size(GROUP_AXIS)
    me = lax.axis_index(GROUP_AXIS)
    s_rows, z_zero = single_blk[0], pair_blk[0]
    r = z_zero.shape[0]
    mask_bias = (mask_blk.astype(F32) - 1.0) * MASK_PENALTY
    (mo_in, mo_gate, mo_proj, mi_in, mi_gate, mi_proj, st_qkvg, st_tb, st_o, en_qkvg, en_tb, en_o, p_up, p_down,
     g_qkvg, g_qb, g_pb, g_o, g_up, g_down) = weights
    tri_heads, single_heads = st_tb.shape[1], g_pb.shape[1]
    st_t, en_t, pb_t = pad_bias(st_tb), pad_bias(en_tb), g_pb.T
    total = sum(w.size for w in weights)

    both = gather_rows(jnp.stack([s_rows, d_single_blk[0]], axis=1))
    s_all, ds_all = both[:, 0], both[:, 1]
    d_pair_recv = exchange(d_pair_blk[0])

    left1, right1 = mul_pre(z_zero, mo_in, False)
    right1_g = gather(right1)
    z_one, xh1, xhat1, rstd1, _ = mul_post(left1, right1_g, z_zero, mo_gate, mo_proj, st_t, False)
    left1_g = gather(left1)
    left2, right2, left2_nat = mul_pre(z_one, mi_in, True)
    z_two, xh2, xhat2, rstd2, bias3 = mul_post(exchange(left2_nat), gather(right2), z_one, mi_gate, mi_proj, st_t, True)
    bias3_g = gather_rows(bias3)
    z_three = att_fwd(z_two, bias3_g, mask_bias, st_qkvg, st_o, tri_heads)
    zc_three, bias4 = turn(exchange(z_three), en_t)
    bias4_g = gather_rows(bias4)
    zc_four = att_fwd(zc_three, bias4_g, mask_bias, en_qkvg, en_o, tri_heads)
    zc_five, z_five_turn, pbias = pair_trans(zc_four, p_up, p_down, pb_t)
    z_five = exchange_back(z_five_turn)
    s_new, ds_in, d_pb, single_grads = single_track(
        s_all, ds_all, gather_rows(pbias), mask_bias.reshape(-1, 1), g_qkvg, g_qb.reshape(1, -1), g_o, g_up, g_down,
        single_heads)
    n_pair = sum(w.size for w in weights[:14]) // 128
    own_single = reduce_single(single_grads, n_pair, total)
    d_pb_own = lax.dynamic_slice_in_dim(d_pb, me * r, r, 1).transpose(1, 0, 2)
    dzc_four, d_pup, d_pdown, d_pbt = pair_trans_back(d_pair_recv, zc_five, d_pb_own, zc_four, p_up, p_down, pb_t)
    dz_part4, d_bias4, d_enq, d_eno = att_back(dzc_four, zc_three, bias4_g, mask_bias, en_qkvg, en_o, tri_heads)
    n = z_zero.shape[1]
    db4 = reduce_bias(d_bias4.reshape(tri_heads, n, n), tri_heads, group)
    dz_three_turn, d_ent = bias_back(dz_part4, zc_three, db4, en_t, True)
    dz_three = exchange_back(dz_three_turn)
    dz_part3, d_bias3, d_stq, d_sto = att_back(dz_three, z_two, bias3_g, mask_bias, st_qkvg, st_o, tri_heads)
    db3 = reduce_bias(d_bias3.reshape(tri_heads, n, n), tri_heads, group)
    dz_two, d_stt = bias_back(dz_part3, z_two, db3, st_t, False)
    dm2, dgp2, d_mip = mul_back_post(dz_two, z_one, xh2, xhat2, rstd2, mi_gate, mi_proj, False)
    dz_one, d_mii, d_mig = mul_back_pre(dz_two, z_one, dgp2, gather(dm2), left2, right2, mask_bias, mi_in, mi_gate, True)
    dm1, dgp1, d_mop, dm1_nat = mul_back_post(dz_one, z_zero, xh1, xhat1, rstd1, mo_gate, mo_proj, True)
    dz_zero, d_moi, d_mog = mul_back_pre(dz_one, z_zero, dgp1, dm1, exchange(dm1_nat), right1_g, left1_g, mo_in, mo_gate,
                                         False)
    flat = [d_moi, d_mog, d_mop, d_mii, d_mig, d_mip, d_stq, bias_grad(d_stt, tri_heads), d_sto,
            d_enq, bias_grad(d_ent, tri_heads), d_eno, d_pup, d_pdown]
    pair_rows = jnp.concatenate([g.reshape(-1, 128) for g in flat])
    pb_row = n_pair + (g_qkvg.size + g_qb.size) // 128
    grad_flat = finish_grads(own_single, pair_rows, bias_grad(d_pbt, single_heads), pb_row, total)
    s_out = lax.dynamic_slice_in_dim(s_new, me * r, r, 0)
    ds_out = lax.dynamic_slice_in_dim(ds_in, me * r, r, 0)
    return s_out[None], z_five[None], ds_out[None], dz_zero[None], grad_flat


def solution(mesh):
    spec_single = P(BATCH_AXIS, GROUP_AXIS, None)
    spec_pair = P(BATCH_AXIS, GROUP_AXIS, None, None)
    spec_mask = P(BATCH_AXIS, None)

    def block_fn(single_rep, pair_rep, token_mask, d_single_out, d_pair_out, *weights):
        in_specs = (spec_single, spec_pair, spec_mask, spec_single, spec_pair) + tuple(P() for w_item in weights)
        out_specs = (spec_single, spec_pair, spec_single, spec_pair, P(BATCH_AXIS))
        mapped = jax.shard_map(device_step, mesh=mesh, in_specs=in_specs, out_specs=out_specs, check_vma=False)
        return mapped(single_rep, pair_rep, token_mask, d_single_out, d_pair_out, *weights)

    return block_fn
```

time: 1360 us -> 834 us (0.61)
  blocking collectives: 535 us -> 55.5 us
  Pallas kernels: 0 us -> 293 us
  local copies, waits for them, and re-layouts: 259 us -> 59.1 us
  matrix products: 196 us -> 0 us
  waiting for transfers between devices: 229 us -> 375 us
  other arithmetic: 79 us -> 4.87 us
    unnamed x3 -> x0, blocking collectives: 507 us -> none
    pallas_call x0 -> x18, Pallas kernels: none -> 293 us  [call(): pl.pallas_call(body, out_shape=outs, scratch_shapes=scratch, name=name, i...]
    dot_general x79 -> x0, matrix products: 179 us -> none  [the longest x6 24.9 us: att_pre(): proj_all = jnp.dot(normed, w_qkvg, preferred_element_type=jnp.float32)]
    unnamed x509 -> x44, local copies, waits for them, and re-layouts: 122 us -> 12.2 us
    all_gather x2 -> x6, waiting for transfers between devices: 47.8 us -> 106 us  [the longest x4 82.8 us: gather(): return lax.all_gather(x, GROUP_AXIS, axis=0, tiled=False)]
    reduce_scatter x4 -> x3, waiting for transfers between devices: 68.5 us -> 117 us  [the longest x1 76.9 us: reduce_single(): lax.psum_scatter(jnp.concatenate(pieces), BATCH_AXIS, scatter_dimension=0...]
    psum x1, waiting for transfers between devices: 36.7 us -> 69.6 us  [finish_grads(): rows = gather_rows(lax.psum(rows, BATCH_AXIS))]
    unnamed x7 -> x12, waiting for transfers between devices: 0.11 us -> 28.6 us
  transfers between devices with their start and end apart: 13 -> 16, of which waited for: 10 -> 13; matrix products, arithmetic and copies ran while one was open for 9% -> 4% of each run, Pallas kernels for 0% -> 8%
where the time goes in v1:
time: 834 us; the launch traced here: 820 us
  waiting for transfers between devices  375 us (45%)
  Pallas kernels  293 us (35%)
  local copies, waits for them, and re-layouts  59.1 us (7%)
  blocking collectives  55.5 us (7%)
  starting transfers between devices  18.2 us (2%)
  between operations  14.6 us (2%)
    pallas_call x18, Pallas kernels, call(): pl.pallas_call(body, out_shape=outs, scratch_shapes=scratch, name=name, i...  293 us
    all_gather x4, waiting for transfers between devices, gather(): return lax.all_gather(x, GROUP_AXIS, axis=0, tiled=False)  82.8 us
    reduce_scatter x1, waiting for transfers between devices, reduce_single(): lax.psum_scatter(jnp.concatenate(pieces), BATCH_AXIS, scatter_dimension=0...  76.9 us
    psum x1, waiting for transfers between devices, finish_grads(): rows = gather_rows(lax.psum(rows, BATCH_AXIS))  69.6 us
    reduce_scatter x2, waiting for transfers between devices, reduce_bias(): own = lax.psum_scatter(parts, GROUP_AXIS, scatter_dimension=0, tiled=False)  40.3 us
    all_gather x4, blocking collectives, gather_rows(): return lax.all_gather(x, GROUP_AXIS, axis=0, tiled=True)  37.6 us
    all_to_all x4, waiting for transfers between devices, exchange(): return lax.all_to_all(x, GROUP_AXIS, 1, 0, tiled=True)  33 us
    unnamed x12, waiting for transfers between devices  28.6 us
  transfers between devices with their start and end apart: 16, of which 13 were waited for; matrix products, arithmetic and copies ran while one was open for 4% of the time, Pallas kernels for 8%

profile of v1, /device:TPU:0, one launch (start us, length us, event | category | flops | bytes accessed | tf_op | source)
XLA Modules:
  0.0 820.2 jit_solution(14524125936967801309)
XLA Ops:
  7.2 8.7 %mul_pre_out.1 = (bf16[128,32,128]{2,1,0:T(8,128)(2,1)}, bf16[128,32,128]{2,1,0:T(8,128)(2,1)}) custom-call(bf16[32,128,128]{2,1,0:T(8,128)(2,1)} %bitcast.80, bf16[128,512]{1,0:T(8,128)(2,1)} %w_in.7), custom_call_target="tpu_custom_call" | custom-call | tf_op jit(solution)/shard_map/mul_pre_out/pallas_call | solution.py:76
  16.0 1.3 pad.30.w_tb.w_t
  17.2 35.9 %all-gather.15.cloned.1.call-done = bf16[512,32,128]{2,1,0:T(8,128)(2,1)} async-done(((bf16[128,32,128]{2,1,0:T(8,128)(2,1)}), bf16[512,32,128]{2,1,0:T(8,128)(2,1)}) %all-gather.15.cloned.1.call-update) | async-done | bytes 4194320 | tf_op jit(solution)/shard_map/all_gather | solution.py:653
  53.1 15.4 %mul_post_out.1 = (bf16[32,128,128]{2,1,0:T(8,128)(2,1)}, bf16[32,128,128]{2,1,0:T(8,128)(2,1)}, f32[128,32,128]{2,1,0:T(8,128)}, f32[32,128]{1,0:T(8,128)}, bf16[32,16,128]{2,1,0:T(8,128)(2,1)}) custom-call(bf16[128,32,128]{2,1,0:T(8,128)(2,1)} %get-tuple-element.57.left, bf16[4,128,32,128]{3,2,1,0:T(8,128)(2,1)} %bitcast.78, ...), custom_call_target="tpu_custom_call" | custom-call | tf_op jit(solution)/shard_map/mul_post_out/pallas_call | solution.py:76
  68.5 9.1 %mul_pre_in.1 = (bf16[128,32,128]{2,1,0:T(8,128)(2,1)}, bf16[128,32,128]{2,1,0:T(8,128)(2,1)}, bf16[32,128,128]{2,1,0:T(8,128)(2,1)}) custom-call(bf16[32,128,128]{2,1,0:T(8,128)(2,1)} %get-tuple-element.59.z, bf16[128,512]{1,0:T(8,128)(2,1)} %w_in.6), custom_call_target="tpu_custom_call" | custom-call | tf_op jit(solution)/shard_map/mul_pre_in/pallas_call | solution.py:76
  77.6 2.9 copy.51
  80.5 3.6 all-to-all-start
  84.2 1.6 copy.75
  85.8 23.2 %all-to-all-done = bf16[32,128,128]{2,0,1:T(8,128)(2,1)S(1)} async-done(((bf16[32,128,128]{2,0,1:T(8,128)(2,1)}), bf16[32,128,128]{2,0,1:T(8,128)(2,1)S(1)}, u32[]{:S(2)}, u32[]{:S(2)}) %all-to-all-start) | async-done | bytes 1048608 | tf_op jit(solution)/shard_map/all_to_all | solution.py:661
  109.0 3.5 all-to-all-start.3
  113.1 1.4 copy.52
  114.6 13.1 %all-gather.17.cloned.1.call-done = bf16[512,32,128]{2,1,0:T(8,128)(2,1)} async-done(((bf16[128,32,128]{2,1,0:T(8,128)(2,1)}), bf16[512,32,128]{2,1,0:T(8,128)(2,1)}) %all-gather.17.cloned.1.call-update) | async-done | bytes 4194320 | tf_op jit(solution)/shard_map/all_gather | solution.py:653
  127.6 18.2 %mul_post_in.1 = (bf16[32,128,128]{2,1,0:T(8,128)(2,1)}, bf16[32,128,128]{2,1,0:T(8,128)(2,1)}, f32[128,32,128]{2,1,0:T(8,128)}, f32[32,128]{1,0:T(8,128)}, bf16[32,16,128]{2,1,0:T(8,128)(2,1)}) custom-call(bf16[128,32,128]{2,1,0:T(8,128)(2,1)} %bitcast.96, bf16[4,128,32,128]{3,2,1,0:T(8,128)(2,1)} %bitcast.86, bf16[32,128,128]{2,1,0:T(8,128)(2,1)} %get-tuple-element.59.z, ...), custom_call_target="tpu_custom_call" | custom-call | tf_op jit(solution)/shard_map/mul_post_in/pallas_call | solution.py:76
  145.8 7.4 all_gather.47.bias_g
  153.2 13.4 %att_fwd.2 = bf16[32,128,128]{2,1,0:T(8,128)(2,1)} custom-call(bf16[32,128,128]{2,1,0:T(8,128)(2,1)} %get-tuple-element.62.z, bf16[128,16,128]{2,1,0:T(8,128)(2,1)} %all_gather.47.bias_g, f32[1,128]{1,0:T(1,128)} %get-tuple-element.112.mask.opd, bf16[128,512]{1,0:T(8,128)(2,1)} %w_qkvg.9, bf16[128,128]{1,0:T(8,128)(2,1)} %w_o.9), custom_call_target="tpu_custom_call" | custom-call | tf_op jit(solution)/shard_map/att_fwd/pallas_call | solution.py:76
  166.6 2.9 copy.53
  169.5 3.5 all-to-all-start.1
  175.0 14.1 %all_gather.42 = bf16[128,2,384]{2,0,1:T(8,128)(2,1)S(1)} all-gather(bf16[32,2,384]{2,0,1:T(8,128)(2,1)S(1)} %pad_maximum_fusion), channel_id=1, replica_groups=mesh['dp'=8,'dap'=4] {'dap'}, dimensions={0}, use_global_device_ids=true | all-gather | bytes 245760 | tf_op jit(solution)/shard_map/all_gather | solution.py:657
  189.8 1.4 copy.58
  191.2 1.4 copy.54
  192.5 5.4 turn.1
  197.9 7.6 all_gather.48.bias_g
  205.5 13.4 %att_fwd.3.z = bf16[32,128,128]{2,1,0:T(8,128)(2,1)} custom-call(bf16[32,128,128]{2,1,0:T(8,128)(2,1)} %get-tuple-element.64.z, bf16[128,16,128]{2,1,0:T(8,128)(2,1)} %all_gather.48.bias_g, f32[1,128]{1,0:T(1,128)} %get-tuple-element.112.mask.opd, bf16[128,512]{1,0:T(8,128)(2,1)} %w_qkvg.8, bf16[128,128]{1,0:T(8,128)(2,1)} %w_o.8), custom_call_target="tpu_custom_call" | custom-call | tf_op jit(solution)/shard_map/att_fwd/pallas_call | solution.py:76
  218.8 12.3 %pair_trans.1 = (bf16[32,128,128]{2,1,0:T(8,128)(2,1)}, bf16[128,32,128]{2,1,0:T(8,128)(2,1)}, bf16[32,16,128]{2,1,0:T(8,128)(2,1)}) custom-call(bf16[32,128,128]{2,1,0:T(8,128)(2,1)} %att_fwd.3.z, bf16[128,1024]{1,0:T(8,128)(2,1)} %w_up.5, bf16[512,128]{1,0:T(8,128)(2,1)} %w_down.5, bf16[16,128]{1,0:T(8,128)(2,1)} %bitcast.105), custom_call_target="tpu_custom_call" | custom-call | tf_op jit(solution)/shard_map/pair_trans/pallas_call | solution.py:76
  231.2 8.6 %all_gather.49.pb_g = bf16[128,16,128]{2,1,0:T(8,128)(2,1)} all-gather(bf16[32,16,128]{2,1,0:T(8,128)(2,1)} %get-tuple-element.66), channel_id=1, replica_groups=mesh['dp'=8,'dap'=4] {'dap'}, dimensions={0}, use_global_device_ids=true | all-gather | bytes 655360 | tf_op jit(solution)/shard_map/all_gather | solution.py:657
  239.8 27.9 %single_track.1 = (bf16[128,384]{1,0:T(8,128)(2,1)}, bf16[128,384]{1,0:T(8,128)(2,1)}, bf16[16,128,128]{2,1,0:T(8,128)(2,1)}, f32[19603,128]{1,0:T(8,128)}) custom-call(bf16[128,384]{1,0:T(8,128)(2,1)} %get-tuple-element.110.s, bf16[128,384]{1,0:T(8,128)(2,1)} %get-tuple-element.109.ds, bf16[128,16,128]{2,1,0:T(8,128)(2,1)} %all_gather.49.pb_g, ...), custom_call_target="tpu_custom_call" | custom-call | tf_op jit(solution)/shard_map/single_track/pallas_call | solution.py:76
  267.7 1.4 copy.59
  269.7 19.4 %pair_trans_back.1 = (bf16[32,128,128]{2,1,0:T(8,128)(2,1)}, f32[128,1024]{1,0:T(8,128)}, f32[512,128]{1,0:T(8,128)}, f32[16,128]{1,0:T(8,128)}) custom-call(bf16[128,32,128]{2,1,0:T(8,128)(2,1)} %bitcast.95, bf16[32,128,128]{2,1,0:T(8,128)(2,1)} %get-tuple-element.70.z5, bf16[32,16,128]{2,1,0:T(8,128)(2,1)} %dynamic-slice_bitcast_fusion.db, ...), custom_call_target="tpu_custom_call" | custom-call | tf_op jit(solution)/shard_map/pair_trans_back/pallas_call | solution.py:76
  289.2 37.0 %att_back.2 = (f32[32,128,128]{2,1,0:T(8,128)}, f32[512,128]{1,0:T(8,128)}, f32[128,512]{1,0:T(8,128)}, f32[128,128]{1,0:T(8,128)}) custom-call(bf16[32,128,128]{2,1,0:T(8,128)(2,1)} %get-tuple-element.72.dz, bf16[32,128,128]{2,1,0:T(8,128)(2,1)} %get-tuple-element.64.z, bf16[128,16,128]{2,1,0:T(8,128)(2,1)} %all_gather.48.bias_g, ...), custom_call_target="tpu_custom_call" | custom-call | tf_op jit(solution)/shard_map/att_back/pallas_call | solution.py:76
  326.1 1.7 copy.60
  327.9 20.1 %reduce-scatter.7.cloned.1.call-done = f32[1,4,32,128]{3,2,1,0:T(8,128)} async-done(((f32[4,4,32,128]{3,2,1,0:T(8,128)}), f32[1,4,32,128]{3,2,1,0:T(8,128)}) %reduce-scatter.7.cloned.1.call-update) | async-done | bytes 65552 | tf_op jit(solution)/shard_map/reduce_scatter | solution.py:671
  349.5 6.9 bias_back.2
  356.4 17.9 %all_to_all.105 = bf16[128,32,128]{2,1,0:T(8,128)(2,1)S(1)} all-to-all(bf16[128,32,128]{2,1,0:T(8,128)(2,1)} %get-tuple-element.75), channel_id=1, replica_groups=mesh['dp'=8,'dap'=4] {'dap'}, dimensions={0} | all-to-all | bytes 2097152 | tf_op jit(solution)/shard_map/all_to_all | solution.py:665
  375.4 37.0 %att_back.3 = (f32[32,128,128]{2,1,0:T(8,128)}, f32[512,128]{1,0:T(8,128)}, f32[128,512]{1,0:T(8,128)}, f32[128,128]{1,0:T(8,128)}) custom-call(bf16[32,128,128]{2,1,0:T(8,128)(2,1)} %bitcast.92, bf16[32,128,128]{2,1,0:T(8,128)(2,1)} %get-tuple-element.62.z, bf16[128,16,128]{2,1,0:T(8,128)(2,1)} %all_gather.47.bias_g, f32[1,128]{1,0:T(1,128)} %get-tuple-element.112.mask.opd, ...), custom_call_target="tpu_custom_call" | custom-call | tf_op jit(solution)/shard_map/att_back/pallas_call | solution.py:76
  412.4 1.7 copy.63
  414.2 20.2 %reduce-scatter.9.cloned.1.call-done = f32[1,4,32,128]{3,2,1,0:T(8,128)} async-done(((f32[4,4,32,128]{3,2,1,0:T(8,128)}), f32[1,4,32,128]{3,2,1,0:T(8,128)}) %reduce-scatter.9.cloned.1.call-update) | async-done | bytes 65552 | tf_op jit(solution)/shard_map/reduce_scatter | solution.py:671
  435.9 6.4 bias_back.3
  442.3 11.3 %mul_back_post.2 = (bf16[128,32,128]{2,1,0:T(8,128)(2,1)}, bf16[32,128,128]{2,1,0:T(8,128)(2,1)}, f32[128,128]{1,0:T(8,128)}) custom-call(bf16[32,128,128]{2,1,0:T(8,128)(2,1)} %get-tuple-element.78.dz, bf16[32,128,128]{2,1,0:T(8,128)(2,1)} %get-tuple-element.59.z, bf16[32,128,128]{2,1,0:T(8,128)(2,1)} %get-tuple-element.79.xh_nat, ...), custom_call_target="tpu_custom_call" | custom-call | tf_op jit(solution)/shard_map/mul_back_post/pallas_call | solution.py:76
  454.2 33.9 %all-gather.19.cloned.1.call-done = bf16[512,32,128]{2,1,0:T(8,128)(2,1)} async-done(((bf16[128,32,128]{2,1,0:T(8,128)(2,1)}), bf16[512,32,128]{2,1,0:T(8,128)(2,1)}) %all-gather.19.cloned.1.call-update) | async-done | bytes 4194320 | tf_op jit(solution)/shard_map/all_gather | solution.py:653
  488.0 18.6 %mul_back_pre_in.1 = (bf16[32,128,128]{2,1,0:T(8,128)(2,1)}, f32[128,512]{1,0:T(8,128)}, f32[128,128]{1,0:T(8,128)}) custom-call(bf16[32,128,128]{2,1,0:T(8,128)(2,1)} %get-tuple-element.78.dz, bf16[32,128,128]{2,1,0:T(8,128)(2,1)} %get-tuple-element.59.z, bf16[32,128,128]{2,1,0:T(8,128)(2,1)} %get-tuple-element.82.dgp, bf16[4,128,32,128]{3,2,1,0:T(8,128)(2,1)} %bitcast.84, ...), custom_call_target="tpu_custom_call" | custom-call | tf_op jit(solution)/shard_map/mul_back_pre_in/pallas_call | solution.py:76
  506.6 12.4 %mul_back_post.3 = (bf16[128,32,128]{2,1,0:T(8,128)(2,1)}, bf16[32,128,128]{2,1,0:T(8,128)(2,1)}, f32[128,128]{1,0:T(8,128)}, bf16[32,128,128]{2,1,0:T(8,128)(2,1)}) custom-call(bf16[32,128,128]{2,1,0:T(8,128)(2,1)} %get-tuple-element.85.dz, bf16[32,128,128]{2,1,0:T(8,128)(2,1)} %bitcast.82, bf16[32,128,128]{2,1,0:T(8,128)(2,1)} %get-tuple-element.86.xh_nat, ...), custom_call_target="tpu_custom_call" | custom-call | tf_op jit(solution)/shard_map/mul_back_post/pallas_call | solution.py:76
  519.1 3.0 copy.65
  522.0 3.5 all-to-all-start.5
  529.9 9.8 %all-to-all-done.5 = bf16[32,128,128]{2,0,1:T(8,128)(2,1)S(1)} async-done(((bf16[32,128,128]{2,0,1:T(8,128)(2,1)}), bf16[32,128,128]{2,0,1:T(8,128)(2,1)S(1)}, u32[]{:S(2)}, u32[]{:S(2)}) %all-to-all-start.5) | async-done | bytes 1048608 | tf_op jit(solution)/shard_map/all_to_all | solution.py:661
  539.8 1.4 copy.66
  541.1 20.0 %mul_back_pre_out.1 = (bf16[32,128,128]{2,1,0:T(8,128)(2,1)}, f32[128,512]{1,0:T(8,128)}, f32[128,128]{1,0:T(8,128)}) custom-call(bf16[32,128,128]{2,1,0:T(8,128)(2,1)} %get-tuple-element.85.dz, bf16[32,128,128]{2,1,0:T(8,128)(2,1)} %bitcast.83, bf16[32,128,128]{2,1,0:T(8,128)(2,1)} %get-tuple-element.89.dgp, bf16[128,32,128]{2,1,0:T(8,128)(2,1)} %get-tuple-element.90.opa, ...), custom_call_target="tpu_custom_call" | custom-call | tf_op jit(solution)/shard_map/mul_back_pre_out/pallas_call | solution.py:76
  561.2 1.7 reshape.48
  562.8 9.0 %concatenate.7 = f32[4376,128]{1,0:T(8,128)S(1)} concatenate(f32[512,128]{1,0:T(8,128)} %reshape.48, f32[128,128]{1,0:T(8,128)} %get-tuple-element.95, f32[128,128]{1,0:T(8,128)} %get-tuple-element.96, f32[512,128]{1,0:T(8,128)S(1)} %reshape.49, f32[128,128]{1,0:T(8,128)} %get-tuple-element.98, f32[128,128]{1,0:T(8,128)} %get-tuple-element.99, f32[512,128]{1,0:T(8,128)S(1)} %reshape.50, ...), dimensions={0} | concatenate | bytes 4481024 | tf_op jit(solution)/shard_map/concatenate | solution.py:704
  571.9 1.6 pad.35
  574.0 1.7 slice-done
  575.7 1.3 slice-done.1
  577.7 27.9 %reduce-scatter.13.cloned.1.call-done = f32[1096,128]{1,0:T(8,128)} async-done(((f32[4384,128]{1,0:T(8,128)}), f32[1096,128]{1,0:T(8,128)}) %reduce-scatter.13.cloned.1.call-update) | async-done | bytes 561168
  605.7 1.4 fusion.6
  607.1 1.9 fusion.7
  610.7 1.6 copy-done
  612.4 69.6 %all-reduce.11.cloned.1.call-done = f32[1096,128]{1,0:T(8,128)} async-done(((f32[1096,128]{1,0:T(8,128)}), f32[1096,128]{1,0:T(8,128)}) %all-reduce.11.cloned.1.call-update) | async-done | bytes 561168 | tf_op jit(solution)/shard_map/psum | solution.py:707
  682.1 76.9 %reduce-scatter.11.cloned.1.call-done = f32[752,128]{1,0:T(8,128)} async-done(((f32[6016,128]{1,0:T(8,128)}), f32[752,128]{1,0:T(8,128)}) %reduce-scatter.11.cloned.1.call-update) | async-done | bytes 385040 | tf_op jit(solution)/shard_map/reduce_scatter | solution.py:696
  759.0 3.5 all-to-all-start.2
  762.5 1.4 dynamic-slice_bitcast_fusion.1
  763.9 20.9 %all-to-all-done.2 = bf16[128,32,128]{2,1,0:T(8,128)(2,1)S(1)} async-done(((bf16[128,32,128]{2,1,0:T(8,128)(2,1)}), bf16[128,32,128]{2,1,0:T(8,128)(2,1)S(1)}, u32[]{:S(2)}, u32[]{:S(2)}) %all-to-all-start.2) | async-done | bytes 1048608 | tf_op jit(solution)/shard_map/all_to_all | solution.py:665
  786.0 4.2 all-gather.13.cloned.1.call-done
  790.2 18.9 %all-gather.11.cloned.1.call-done = f32[3008,128]{1,0:T(8,128)} async-done(((f32[752,128]{1,0:T(8,128)}), f32[3008,128]{1,0:T(8,128)}) %all-gather.11.cloned.1.call-update) | async-done | bytes 1540112 | tf_op jit(solution)/shard_map/all_gather | solution.py:657
  809.1 2.6 fusion.1
  811.7 1.6 dynamic_slice.55
  (95 shorter events, 17.5 us)
Async XLA Ops:
  7.2 45.9 %all-gather.15.cloned.1.call-start = ((), (), s32[]{:S(2)}) async-start(), calls=%async_computation.16 | async-start | bytes 5242880 | tf_op jit(solution)/shard_map/all_gather | solution.py:653
  15.9 111.7 %all-gather.17.cloned.1.call-start = ((), (), s32[]{:S(2)}) async-start(), calls=%async_computation.17 | async-start | bytes 5242880 | tf_op jit(solution)/shard_map/all_gather | solution.py:653
  68.5 15.7 %copy-start.1 = (bf16[1,32,128,128]{3,2,1,0:T(8,128)(2,1)S(1)}, bf16[1,32,128,128]{3,2,1,0:T(8,128)(2,1)}, u32[]{:S(2)}) copy-start(bf16[1,32,128,128]{3,2,1,0:T(8,128)(2,1)} %param.29) | copy-start | bytes 3145732
  80.5 32.1 %copy-start.10 = (s32[1,128]{1,0:T(1,128)S(1)}, s32[1,128]{1,0:T(1,128)}, u32[]{:S(2)}) copy-start(s32[1,128]{1,0:T(1,128)} %param.27) | copy-start | bytes 1540
  80.5 28.5 %all-to-all-start = ((bf16[32,128,128]{2,0,1:T(8,128)(2,1)}), bf16[32,128,128]{2,0,1:T(8,128)(2,1)S(1)}, u32[]{:S(2)}, u32[]{:S(2)}) async-start(bf16[32,128,128]{2,0,1:T(8,128)(2,1)} %copy.51), calls=%async_computation | async-start | bytes 2097152 | tf_op jit(solution)/shard_map/all_to_all | solution.py:661
  109.0 60.4 %all-to-all-start.3 = ((bf16[32,128,128]{2,0,1:T(8,128)(2,1)}), bf16[32,128,128]{2,0,1:T(8,128)(2,1)S(1)}, u32[]{:S(2)}, u32[]{:S(2)}) async-start(bf16[32,128,128]{2,0,1:T(8,128)(2,1)} %bitcast.71), calls=%async_computation.3 | async-start | bytes 2097152 | tf_op jit(solution)/shard_map/all_to_all | solution.py:661
  153.2 19.9 %copy-start.9 = (bf16[128,4]{0,1:T(4,128)(2,1)S(1)}, bf16[128,4]{0,1:T(4,128)(2,1)}, u32[]{:S(2)}) copy-start(bf16[128,4]{0,1:T(4,128)(2,1)} %param.40) | copy-start | bytes 3076
  153.2 21.2 %copy-start.8 = (bf16[384]{0:T(512)(128)(2,1)S(1)}, bf16[384]{0:T(512)(128)(2,1)}, u32[]{:S(2)}) copy-start(bf16[384]{0:T(512)(128)(2,1)} %param.45) | copy-start | bytes 2308
  153.2 21.8 %copy-start.5 = (bf16[1,32,384]{2,1,0:T(8,128)(2,1)S(1)}, bf16[1,32,384]{2,1,0:T(8,128)(2,1)}, u32[]{:S(2)}) copy-start(bf16[1,32,384]{2,1,0:T(8,128)(2,1)} %param.28) | copy-start | bytes 73732
  153.2 21.8 %copy-start.6 = (bf16[1,32,384]{2,1,0:T(8,128)(2,1)S(1)}, bf16[1,32,384]{2,1,0:T(8,128)(2,1)}, u32[]{:S(2)}) copy-start(bf16[1,32,384]{2,1,0:T(8,128)(2,1)} %param.25) | copy-start | bytes 73732
  169.5 21.7 %all-to-all-start.1 = ((bf16[32,128,128]{2,0,1:T(8,128)(2,1)}), bf16[32,128,128]{2,0,1:T(8,128)(2,1)S(1)}, u32[]{:S(2)}, u32[]{:S(2)}) async-start(bf16[32,128,128]{2,0,1:T(8,128)(2,1)} %copy.53), calls=%async_computation.1 | async-start | bytes 2097152 | tf_op jit(solution)/shard_map/all_to_all | solution.py:661
  173.0 175.0 %reduce-scatter.7.cloned.1.call-start = ((), (), s32[]{:S(2)}) async-start(), calls=%async_computation.10 | async-start | bytes 327680 | tf_op jit(solution)/shard_map/reduce_scatter | solution.py:671
  327.8 106.5 %reduce-scatter.9.cloned.1.call-start = ((), (), s32[]{:S(2)}) async-start(), calls=%async_computation.11 | async-start | bytes 327680 | tf_op jit(solution)/shard_map/reduce_scatter | solution.py:671
  414.1 73.9 %all-gather.19.cloned.1.call-start = ((), (), s32[]{:S(2)}) async-start(), calls=%async_computation.18 | async-start | bytes 5242880 | tf_op jit(solution)/shard_map/all_gather | solution.py:653
  453.6 87.5 %all-gather.21.cloned.1.call-start = ((), (), s32[]{:S(2)}) async-start(), calls=%async_computation.19 | async-start | bytes 5242880 | tf_op jit(solution)/shard_map/all_gather | solution.py:653
  519.1 6.6 copy-start.3
  519.1 6.6 copy-start.2
  519.1 6.7 copy-start.7
  519.1 8.4 %copy-start.4 = (f32[128,512]{1,0:T(8,128)S(1)}, f32[128,512]{1,0:T(8,128)}, u32[]{:S(2)}) copy-start(f32[128,512]{1,0:T(8,128)} %get-tuple-element.100) | copy-start | bytes 786436
  522.0 17.7 %all-to-all-start.5 = ((bf16[32,128,128]{2,0,1:T(8,128)(2,1)}), bf16[32,128,128]{2,0,1:T(8,128)(2,1)S(1)}, u32[]{:S(2)}, u32[]{:S(2)}) async-start(bf16[32,128,128]{2,0,1:T(8,128)(2,1)} %copy.65), calls=%async_computation.7 | async-start | bytes 2097152 | tf_op jit(solution)/shard_map/all_to_all | solution.py:661
  525.6 80.0 %reduce-scatter.13.cloned.1.call-start = ((), (), s32[]{:S(2)}) async-start(), calls=%async_computation.20 | async-start | bytes 2805760
  573.5 108.5 %all-reduce.11.cloned.1.call-start = ((), (), s32[]{:S(2)}) async-start(), calls=%async_computation.14 | async-start | bytes 1122304 | tf_op jit(solution)/shard_map/psum | solution.py:707
  573.6 2.2 slice-start
  573.6 3.5 slice-start.1
  573.8 3.7 slice-start.2
  605.6 153.3 %reduce-scatter.11.cloned.1.call-start = ((), (), s32[]{:S(2)}) async-start(), calls=%async_computation.12 | async-start | bytes 3465216 | tf_op jit(solution)/shard_map/reduce_scatter | solution.py:696
  605.7 3.3 slice-start.3
  605.7 3.7 slice-start.4
  607.1 3.0 slice-start.5
  610.7 1.6 copy-start
  612.3 177.8 %all-gather.13.cloned.1.call-start = ((), (), s32[]{:S(2)}) async-start(), calls=%async_computation.15 | async-start | bytes 2805760 | tf_op jit(solution)/shard_map/all_gather | solution.py:657
  682.0 127.1 %all-gather.11.cloned.1.call-start = ((), (), s32[]{:S(2)}) async-start(), calls=%async_computation.13 | async-start | bytes 1925120 | tf_op jit(solution)/shard_map/all_gather | solution.py:657
  759.0 25.9 %all-to-all-start.2 = ((bf16[128,32,128]{2,1,0:T(8,128)(2,1)}), bf16[128,32,128]{2,1,0:T(8,128)(2,1)S(1)}, u32[]{:S(2)}, u32[]{:S(2)}) async-start(bf16[128,32,128]{2,1,0:T(8,128)(2,1)} %get-tuple-element.68), calls=%async_computation.2 | async-start | bytes 2097152 | tf_op jit(solution)/shard_map/all_to_all | solution.py:665
  790.2 18.9 %slice-start.6 = ((f32[4384,128]{1,0:T(8,128)}), f32[16,128]{1,0:T(8,128)S(1)}, s32[]{:S(2)}) async-start(f32[4384,128]{1,0:T(8,128)} %all-gather.13.cloned.1.call-done), calls=%async_computation.27 | async-start | bytes 16384 | tf_op jit(solution)/shard_map/slice | solution.py:711
  790.2 18.9 %slice-start.7 = ((f32[4384,128]{1,0:T(8,128)}), f32[4360,128]{1,0:T(8,128)S(1)}, s32[]{:S(2)}) async-start(f32[4384,128]{1,0:T(8,128)} %all-gather.13.cloned.1.call-done), calls=%async_computation.28 | async-start | bytes 4464640 | tf_op jit(solution)/shard_map/slice | solution.py:709
Sparse Core Ops, SparseCore 0:
  16.0 37.0 all-gather.14
  77.7 49.8 all-gather.16
  327.9 20.0 reduce-scatter.6
  414.2 20.0 reduce-scatter.8
  453.7 34.2 all-gather.18
  490.0 34.2 all-gather.20
  573.6 31.9 reduce-scatter.12
  609.0 72.9 all-reduce.10
  685.6 73.3 reduce-scatter.10
  760.4 29.7 all-gather.12
  791.7 17.3 all-gather.10

commit v2 on v1

v2 whole, which is shorter than its diff:
```python
import functools
import jax
import jax.numpy as jnp
from jax import lax
from jax.experimental import pallas as pl
from jax.experimental.pallas import tpu as pltpu
from jax.sharding import PartitionSpec as P

BATCH_AXIS = 'dp'
GROUP_AXIS = 'dap'
NORM_EPS = 1e-5
MASK_PENALTY = 1.0e9
ROWS_STEP = 4
CHAN_STEP = 8
INTERPRET = False
COST = pl.CostEstimate(flops=80_000_000, bytes_accessed=4_000_000, transcendentals=0)
BF16 = jnp.bfloat16
LANES = 128
ALL = ...
F32 = jnp.float32


def nn(x, y):
    return lax.dot_general(x, y, (((1,), (0,)), ((), ())), preferred_element_type=F32)


def nt(x, y):
    return lax.dot_general(x, y, (((1,), (1,)), ((), ())), preferred_element_type=F32)


def tn(x, y):
    return lax.dot_general(x, y, (((0,), (0,)), ((), ())), preferred_element_type=F32)


def norm_parts(x):
    xf = x.astype(F32)
    cent = xf - jnp.mean(xf, axis=-1, keepdims=True)
    rstd = lax.rsqrt(jnp.mean(cent * cent, axis=-1, keepdims=True) + NORM_EPS)
    return cent * rstd, rstd


def norm_back(xhat, rstd, dn):
    m1 = jnp.mean(dn, axis=-1, keepdims=True)
    m2 = jnp.mean(dn * xhat, axis=-1, keepdims=True)
    return rstd * (dn - m1 - xhat * m2)


def round_bf(x):
    return x.astype(BF16).astype(F32)


def swap_lead(src, dst):
    steps = src.shape[1] // 16

    def body(t, carry):
        at = pl.ds(pl.multiple_of(t * 16, 16), 16)
        dst[at] = jnp.swapaxes(src[:, at, :], 0, 1)
        return carry
    lax.fori_loop(0, steps, body, 0)


def swap_minor(src, dst, step=4):
    def body(t, carry):
        at = pl.ds(t * step, step)
        dst[at] = jnp.swapaxes(src[at], 1, 2)
        return carry
    lax.fori_loop(0, src.shape[0] // step, body, 0)


def rows_loop(count, body):
    def wrapped(t, carry):
        body(t)
        return carry
    lax.fori_loop(0, count, wrapped, 0)


def call(body, outs, scratch, *args, name):
    outs = [jax.ShapeDtypeStruct(s, d) for s, d in outs]
    return pl.pallas_call(
        body, out_shape=outs, scratch_shapes=scratch, name=name, interpret=INTERPRET,
        in_specs=[pl.BlockSpec(memory_space=pltpu.VMEM)] * len(args),
        out_specs=[pl.BlockSpec(memory_space=pltpu.VMEM)] * len(outs),
        cost_estimate=COST,
        compiler_params=pltpu.CompilerParams(vmem_limit_bytes=56 * 1024 * 1024),
    )(*args)


MESH_IDS = pl.DeviceIdType.MESH
DP_SIZE = 8


def partners():
    me = lax.axis_index(GROUP_AXIS)
    sibling = me + 1 - 2 * (me % 2)
    return me, (sibling, (me + 2) % 4, (sibling + 2) % 4)


def send_views(kind, src, dst, group):
    if kind in ('gather', 'rows'):
        rows = src.shape[0]

        def put(d):
            return dst.at[d] if kind == 'gather' else dst.at[pl.ds(pl.multiple_of(d * rows, rows), rows)]
        return (lambda p: src), put
    if kind in ('parts', 'dp_parts'):
        return (lambda p: src.at[p]), (lambda d: dst.at[d])
    if kind == 'dp_gather':
        return (lambda p: src), (lambda d: dst.at[d])
    if kind == 'cols':
        rows, block = src.shape[0], src.shape[1] // group
        return (lambda p: src.at[:, pl.ds(pl.multiple_of(p * block, block), block)],
                lambda d: dst.at[pl.ds(pl.multiple_of(d * rows, rows), rows)])
    block, cols = src.shape[0] // group, src.shape[1]
    return (lambda p: src.at[pl.ds(pl.multiple_of(p * block, block), block)],
            lambda d: dst.at[:, pl.ds(pl.multiple_of(d * cols, cols), cols)])


def landing(kind, x, group=4):
    if kind == 'gather':
        return (group,) + x.shape
    if kind == 'dp_gather':
        return (DP_SIZE,) + x.shape
    if kind in ('parts', 'dp_parts'):
        return x.shape
    if kind == 'rows':
        return (group * x.shape[0],) + x.shape[1:]
    if kind == 'cols':
        return (group * x.shape[0], x.shape[1] // group) + x.shape[2:]
    return (x.shape[0] // group, group * x.shape[1]) + x.shape[2:]


def dp_partners():
    dp = lax.axis_index(BATCH_AXIS)
    return dp, [(dp + o) % DP_SIZE for o in range(1, DP_SIZE)]


class Transfer:
    def __init__(self, kind, src, dst, sends, recvs, local):
        over_dp = kind.startswith('dp')
        axis = BATCH_AXIS if over_dp else GROUP_AXIS
        me, peers = dp_partners() if over_dp else partners()
        get, put = send_views(kind, src, dst, 4)
        self.relay = kind == 'gather'

        def remote(view, slot, link, to):
            return pltpu.make_async_remote_copy(
                src_ref=view, dst_ref=put(slot), send_sem=sends.at[link], recv_sem=recvs.at[link],
                device_id={axis: to}, device_id_type=MESH_IDS)
        self.own = pltpu.make_async_copy(get(me), put(me), local)
        self.copies = [remote(get(p), me, link, p) for link, p in enumerate(peers[:2] if self.relay else peers)]
        if self.relay:
            self.copies.append(remote(put(peers[1]), peers[1], 2, peers[0]))

    def start(self):
        for c in reversed(self.copies[:2] if self.relay else self.copies):
            c.start()
        self.own.start()

    def forward(self):
        if self.relay:
            self.copies[1].wait_recv()
            self.copies[2].start()

    def wait(self):
        self.forward()
        self.own.wait()
        for link, c in enumerate(self.copies):
            if self.relay and link == 1:
                c.wait_send()
            else:
                c.wait()


def enter(over_dp):
    me, peers = partners()
    barrier = pltpu.get_barrier_semaphore()
    ids = [{GROUP_AXIS: p} for p in peers]
    if over_dp:
        ids += [{BATCH_AXIS: p} for p in dp_partners()[1]]
    for to in ids:
        pl.semaphore_signal(barrier, inc=1, device_id=to, device_id_type=MESH_IDS)
    pl.semaphore_wait(barrier, len(ids))


def call_with(body, moves, outs, scratch, *args, name, cid, late=()):
    count = len(moves)
    lands = [jax.ShapeDtypeStruct(landing(k, x), x.dtype) for k, x in moves]
    n_args, n_outs = len(args), len(outs)

    def whole(*refs):
        srcs, ins = refs[:count], refs[count:count + n_args]
        at = count + n_args
        dsts, results = refs[at:at + count], refs[at + count:at + count + n_outs]
        rest = refs[at + count + n_outs:]
        sends, recvs, local = rest[-3:]
        enter(any(k.startswith('dp') for k, x in moves))
        jobs = [Transfer(moves[m][0], srcs[m], dsts[m], sends.at[m], recvs.at[m], local.at[m]) for m in range(count)]
        for job in jobs:
            job.start()
        for m, job in enumerate(jobs):
            if m not in late:
                job.wait()
        body(*[d for m, d in enumerate(dsts) if m not in late], *ins, *results, *rest[:-3])
        for m in late:
            jobs[m].wait()
    res = pl.pallas_call(
        whole, out_shape=lands + [jax.ShapeDtypeStruct(sh, d) for sh, d in outs], name=name, interpret=INTERPRET,
        in_specs=[pl.BlockSpec(memory_space=pltpu.VMEM)] * (count + n_args),
        out_specs=[pl.BlockSpec(memory_space=pltpu.VMEM)] * (count + n_outs),
        scratch_shapes=list(scratch) + [pltpu.SemaphoreType.DMA((count, DP_SIZE)), pltpu.SemaphoreType.DMA((count, DP_SIZE)),
                                        pltpu.SemaphoreType.DMA((count,))],
        cost_estimate=COST,
        compiler_params=pltpu.CompilerParams(vmem_limit_bytes=60 * 1024 * 1024, collective_id=cid, has_side_effects=True),
    )(*[x for k, x in moves], *args)
    return res[:count], res[count:]


def total_body(g, out, work1, work2, work3, full, recv1, recv2, recv3, recv4, sends, recvs):
    me, peers = partners()
    dp = lax.axis_index(BATCH_AXIS)
    z = dp // 2
    y = dp % 2
    core, x = me % 2, me // 2
    y_peer = {BATCH_AXIS: 2 * z + 1 - y, GROUP_AXIS: me}
    z_peers = [{BATCH_AXIS: ((z + o) % 4) * 2 + y, GROUP_AXIS: me} for o in (1, 2, 3)]
    core_peer = {BATCH_AXIS: dp, GROUP_AXIS: peers[0]}
    x_peer = {BATCH_AXIS: dp, GROUP_AXIS: peers[1]}
    barrier = pltpu.get_barrier_semaphore()
    for p in [core_peer, x_peer, y_peer] + z_peers:
        pl.semaphore_signal(barrier, inc=1, device_id=p, device_id_type=MESH_IDS)
    pl.semaphore_wait(barrier, 6)
    n = g.shape[0]
    half, quarter, eighth = n // 2, n // 4, n // 8

    def part(ref, index, size):
        return ref.at[pl.ds(pl.multiple_of(index * size, size), size)]

    def copy(src, dst, slot, to):
        return pltpu.make_async_remote_copy(src_ref=src, dst_ref=dst, send_sem=sends.at[slot], recv_sem=recvs.at[slot],
                                            device_id=to, device_id_type=MESH_IDS)

    def fold(src, index, size, recv, dst, slot, to):
        c = copy(part(src, 1 - index, size), recv, slot, to)
        c.start()
        c.wait()
        dst[ALL] = part(src, index, size)[ALL] + recv[ALL]
    fold(g, core, half, recv1, work1, 0, core_peer)
    fold(work1, x, quarter, recv2, work2, 1, x_peer)
    fold(work2, y, eighth, recv3, work3, 2, y_peer)
    sent = [copy(work3, recv4.at[o], 3 + o, z_peers[o]) for o in range(3)]
    for c in sent:
        c.start()
    for c in sent:
        c.wait()
    place = core * 4 + x * 2 + y
    part(full, place, eighth)[ALL] = work3[ALL] + recv4[0] + recv4[1] + recv4[2]
    for slot, index, size, to in ((6, place, eighth, y_peer), (7, core * 2 + x, quarter, x_peer),
                                  (8, core, half, core_peer)):
        piece = part(full, index, size)
        c = copy(piece, piece, slot, to)
        c.start()
        c.wait()
    out[ALL] = full[ALL]


def total(g, cid):
    n = g.shape[0]

    def buf(k, lead=()):
        return pltpu.VMEM(lead + (n // k, g.shape[1]), F32)
    return pl.pallas_call(
        total_body, out_shape=jax.ShapeDtypeStruct(g.shape, F32), name='total', interpret=INTERPRET,
        in_specs=[pl.BlockSpec(memory_space=pltpu.VMEM)], out_specs=pl.BlockSpec(memory_space=pltpu.VMEM),
        scratch_shapes=[buf(2), buf(4), buf(8), buf(1), buf(2), buf(4), buf(8), buf(8, (3,)),
                        pltpu.SemaphoreType.DMA((9,)), pltpu.SemaphoreType.DMA((9,))],
        cost_estimate=COST,
        compiler_params=pltpu.CompilerParams(collective_id=cid, has_side_effects=True),
    )(g)


def mul_pre_body(keep_left, z, w_in, *refs):
    if keep_left:
        left_t, right_t, left_nat, sa, sb = refs
    else:
        left_t, right_t, sa, sb = refs
    width = w_in.shape[1] // 4

    def step(t):
        at = pl.ds(t * ROWS_STEP, ROWS_STEP)
        zc = z[at].reshape(-1, z.shape[-1])
        normed = norm_parts(zc)[0].astype(BF16)
        proj = nn(normed, w_in[ALL])
        left = (jax.nn.sigmoid(proj[:, width:2 * width]) * proj[:, :width]).astype(BF16)
        right = (jax.nn.sigmoid(proj[:, 3 * width:]) * proj[:, 2 * width:3 * width]).astype(BF16)
        left = left.reshape(ROWS_STEP, -1, width)
        right = right.reshape(ROWS_STEP, -1, width)
        if keep_left:
            left_nat[at] = left
        sa[at] = jnp.swapaxes(left, 1, 2)
        sb[at] = jnp.swapaxes(right, 1, 2)
    rows_loop(z.shape[0] // ROWS_STEP, step)
    swap_lead(sa, left_t)
    swap_lead(sb, right_t)


def mul_pre(z, w_in, keep_left):
    r, n, c = z.shape
    width = w_in.shape[1] // 4
    outs = [((width, r, n), BF16)] * 2 + ([((r, n, width), BF16)] if keep_left else [])
    scratch = [pltpu.VMEM((r, width, n), BF16)] * 2
    return call(functools.partial(mul_pre_body, keep_left), outs, scratch, z, w_in,
                name='mul_pre_in' if keep_left else 'mul_pre_out')


def joined(ref, ch):
    return jnp.concatenate([ref[dev, ch] for dev in range(ref.shape[0])], axis=0)


def mul_post_body(incoming, *refs):
    if incoming:
        left, right_g, z, w_gate, w_out, w_tb, z_new, xh_nat, xhat, rstd, bias, tb, t2, u1, u2, u3, b1, b2 = refs
    else:
        right_g, left, z, w_gate, w_out, z_new, xh_nat, xhat, rstd, tb, t2 = refs
    width = xhat.shape[0]
    if incoming:
        swap_lead(left, u1)
        swap_minor(u1, u2)
        swap_lead(u2, u3)
        left = u3

    def mix(t):
        for s in range(CHAN_STEP):
            ch = t * CHAN_STEP + s
            if incoming:
                xhat[ch] = nn(left[ch], joined(right_g, ch))
            else:
                xhat[ch] = nt(left[ch], joined(right_g, ch))
    rows_loop(width // CHAN_STEP, mix)
    zero = jnp.zeros(xhat.shape[1:], F32)
    total = lax.fori_loop(0, width, lambda ch, acc: acc + xhat[ch], zero)
    mean = total / width
    sq = lax.fori_loop(0, width, lambda ch, acc: acc + (xhat[ch] - mean) * (xhat[ch] - mean), zero)
    inv = lax.rsqrt(sq / width + NORM_EPS)
    rstd[ALL] = inv

    def scale(ch):
        val = (xhat[ch] - mean) * inv
        xhat[ch] = val
        tb[ch] = val.astype(BF16)
    rows_loop(width, scale)
    swap_lead(tb, t2)

    def step(t):
        at = pl.ds(t * ROWS_STEP, ROWS_STEP)
        zc = z[at].reshape(-1, z.shape[-1])
        xh = jnp.swapaxes(t2[at], 1, 2)
        xh_nat[at] = xh
        normed = norm_parts(zc)[0].astype(BF16)
        gate = jax.nn.sigmoid(nn(normed, w_gate[ALL]))
        upd = gate * nn(xh.reshape(-1, width), w_out[ALL])
        znew = (zc.astype(F32) + upd).astype(BF16)
        z_new[at] = znew.reshape(ROWS_STEP, -1, z.shape[-1])
        if incoming:
            bias_rows(znew, w_tb, b1, t)
    rows_loop(z.shape[0] // ROWS_STEP, step)
    if incoming:
        swap_lead(b1, b2)
        bias[ALL] = b2[:bias.shape[0]]


def bias_rows(zc, w_t, bias, t):
    normed = norm_parts(zc)[0].astype(BF16).reshape(ROWS_STEP, -1, zc.shape[-1])
    for s in range(ROWS_STEP):
        bias[t * ROWS_STEP + s] = nt(w_t[ALL], normed[s]).astype(BF16)


def mul_post(left, right, z, w_gate, w_out, w_tb, heads, incoming, cid):
    r, n, c = z.shape
    width = w_out.shape[0]
    outs = [((r, n, c), BF16), ((r, n, width), BF16), ((width, r, n), F32), ((r, n), F32)]
    scratch = [pltpu.VMEM((width, r, n), BF16), pltpu.VMEM((r, width, n), BF16)]
    if incoming:
        outs.append(((heads, r, n), BF16))
        scratch += [pltpu.VMEM((r, n, width), BF16), pltpu.VMEM((r, width, n), BF16), pltpu.VMEM((width, r, n), BF16),
                    pltpu.VMEM((r, 16, n), BF16), pltpu.VMEM((16, r, n), BF16)]
        moves, args = [('cols', left), ('gather', right)], (z, w_gate, w_out, w_tb)
    else:
        moves, args = [('gather', right)], (left, z, w_gate, w_out)
    return call_with(functools.partial(mul_post_body, incoming), moves, outs, scratch, *args, cid=cid,
                     name='mul_post_in' if incoming else 'mul_post_out')


def mul_back_post_body(want_nat, dz, z, xh_nat, xhat, rstd, w_gate, w_out, d_t, dgp, g_out, *refs):
    if want_nat:
        d_nat, td, td2 = refs
    else:
        td, td2 = refs
    width = xhat.shape[0]
    g_out[ALL] = jnp.zeros_like(g_out)

    def step(t):
        at = pl.ds(t * ROWS_STEP, ROWS_STEP)
        zc = z[at].reshape(-1, z.shape[-1])
        dzf = dz[at].reshape(-1, z.shape[-1]).astype(F32)
        xh = xh_nat[at].reshape(-1, width)
        normed = norm_parts(zc)[0].astype(BF16)
        gate = jax.nn.sigmoid(nn(normed, w_gate[ALL]))
        y = nn(xh, w_out[ALL])
        dgp[at] = (dzf * y * gate * (1.0 - gate)).astype(BF16).reshape(ROWS_STEP, -1, z.shape[-1])
        dy = (dzf * gate).astype(BF16)
        g_out[ALL] += tn(xh, dy)
        dxh = nt(dy, w_out[ALL]).astype(BF16).reshape(ROWS_STEP, -1, width)
        td[at] = jnp.swapaxes(dxh, 1, 2)
    rows_loop(z.shape[0] // ROWS_STEP, step)
    swap_lead(td, td2)
    zero = jnp.zeros(xhat.shape[1:], F32)

    def sums(ch, acc):
        d = td2[ch].astype(F32)
        return acc[0] + d, acc[1] + d * xhat[ch]
    s1, s2 = lax.fori_loop(0, width, sums, (zero, zero))
    s1, s2, inv = s1 / width, s2 / width, rstd[ALL]

    def fin(ch):
        d_t[ch] = (inv * (td2[ch].astype(F32) - s1 - xhat[ch] * s2)).astype(BF16)
    rows_loop(width, fin)
    if want_nat:
        swap_lead(d_t, td)
        swap_minor(td, d_nat)


def mul_back_post(dz, z, xh_nat, xhat, rstd, w_gate, w_out, want_nat, cid, extra):
    r, n, c = z.shape
    width = w_out.shape[0]
    outs = [((width, r, n), BF16), ((r, n, c), BF16), ((width, c), F32)]
    if want_nat:
        outs.append(((r, n, width), BF16))
    scratch = [pltpu.VMEM((r, width, n), BF16), pltpu.VMEM((width, r, n), BF16)]
    return call_with(functools.partial(mul_back_post_body, want_nat), extra, outs, scratch, dz, z, xh_nat, xhat, rstd,
                     w_gate, w_out, cid=cid, name='mul_back_post', late=tuple(range(len(extra))))


def mul_back_pre_body(incoming, moved, dz, z, dgp, opa, opb, opc, w_in, w_gate, dz_in, g_in, g_gate, da_t, db_t, da_r,
                      db_r, *scr):
    width = w_in.shape[1] // 4
    if incoming:
        d_g, left_t, right_t = moved, opa, opb
    else:
        d_t, d_recv, right_g, left_g = opa, moved, opb, opc
        u1, u2, u3 = scr
        swap_lead(d_recv, u1)
        swap_minor(u1, u2)
        swap_lead(u2, u3)

    def mix(t):
        for s in range(CHAN_STEP):
            ch = t * CHAN_STEP + s
            if incoming:
                d_all = joined(d_g, ch)
                da_t[ch] = nt(right_t[ch], d_all).astype(BF16)
                db_t[ch] = nn(left_t[ch], d_all).astype(BF16)
            else:
                da_t[ch] = nn(d_t[ch], joined(right_g, ch)).astype(BF16)
                db_t[ch] = nn(u3[ch], joined(left_g, ch)).astype(BF16)
    rows_loop(width // CHAN_STEP, mix)
    swap_lead(da_t, da_r)
    swap_lead(db_t, db_r)
    g_in[ALL] = jnp.zeros_like(g_in)
    g_gate[ALL] = jnp.zeros_like(g_gate)

    def step(t):
        at = pl.ds(t * ROWS_STEP, ROWS_STEP)
        c = z.shape[-1]
        zc = z[at].reshape(-1, c)
        da = jnp.swapaxes(da_r[at], 1, 2).reshape(-1, width).astype(F32)
        db = jnp.swapaxes(db_r[at], 1, 2).reshape(-1, width).astype(F32)
        zhat, inv = norm_parts(zc)
        normed = zhat.astype(BF16)
        proj = nn(normed, w_in[ALL])
        sa = jax.nn.sigmoid(proj[:, width:2 * width])
        sb = jax.nn.sigmoid(proj[:, 3 * width:])
        dproj = jnp.concatenate([
            (da * sa).astype(BF16), (da * proj[:, :width] * sa * (1.0 - sa)).astype(BF16),
            (db * sb).astype(BF16), (db * proj[:, 2 * width:3 * width] * sb * (1.0 - sb)).astype(BF16)], axis=1)
        dg = dgp[at].reshape(-1, c)
        g_in[ALL] += tn(normed, dproj)
        g_gate[ALL] += tn(normed, dg)
        dn = round_bf(nt(dproj, w_in[ALL]) + nt(dg, w_gate[ALL]))
        out = dz[at].reshape(-1, c).astype(F32) + norm_back(zhat, inv, dn)
        dz_in[at] = out.astype(BF16).reshape(ROWS_STEP, -1, c)
    rows_loop(z.shape[0] // ROWS_STEP, step)


def mul_back_pre(moves, dz, z, dgp, opa, opb, opc, w_in, w_gate, incoming, cid):
    r, n, c = z.shape
    width = w_in.shape[1] // 4
    outs = [((r, n, c), BF16), (w_in.shape, F32), (w_gate.shape, F32)]
    scratch = [pltpu.VMEM((width, r, n), BF16)] * 2 + [pltpu.VMEM((r, width, n), BF16)] * 2
    if not incoming:
        scratch += [pltpu.VMEM((r, n, width), BF16), pltpu.VMEM((r, width, n), BF16), pltpu.VMEM((width, r, n), BF16)]
    return call_with(functools.partial(mul_back_pre_body, incoming), moves, outs, scratch, dz, z, dgp, opa, opb, opc,
                     w_in, w_gate, cid=cid, name='mul_back_pre_in' if incoming else 'mul_back_pre_out',
                     late=tuple(range(1, len(moves))))


def head_masks(width, heads):
    lane = lax.broadcasted_iota(jnp.int32, (1, width), 1)
    size = width // heads
    return [(lane >= h * size) & (lane < (h + 1) * size) for h in range(heads)]


def stack_heads(x, masks):
    zero = jnp.zeros_like(x)
    return jnp.concatenate([jnp.where(m, x, zero) for m in masks], axis=0)


def pick_heads(x, masks):
    n = x.shape[0] // len(masks)
    out = x[:n]
    for h in range(1, len(masks)):
        out = jnp.where(masks[h], x[h * n:(h + 1) * n], out)
    return out


def load_bias(bias_g, bias_s, add_mask, heads):
    group, rows = bias_g.shape[0], bias_g.shape[2]
    for h in range(heads):
        for d in range(group):
            at = (h * group + d) * rows
            bias_s[at:at + rows] = bias_g[d, h].astype(F32) + add_mask


def soft(logits):
    top = jnp.max(logits, axis=-1, keepdims=True)
    e = jnp.exp(logits - top)
    return e / jnp.sum(e, axis=-1, keepdims=True)


def att_body(heads, bias_g, z, mask, w_qkvg, w_o, z_new, bias_s):
    width = w_o.shape[0]
    n = z.shape[1]
    masks = head_masks(width, heads)
    scale = (width // heads) ** -0.5
    load_bias(bias_g, bias_s, mask[ALL], heads)

    def step(t):
        at = pl.ds(t * ROWS_STEP, ROWS_STEP)
        zc = z[at].reshape(-1, z.shape[-1])
        normed = norm_parts(zc)[0].astype(BF16)
        proj = nn(normed, w_qkvg[ALL])
        qkv = proj[:, :3 * width].astype(BF16)
        outs = []
        for s in range(ROWS_STEP):
            row = qkv[s * n:(s + 1) * n]
            q, k, v = row[:, :width], row[:, width:2 * width], row[:, 2 * width:]
            prob = soft(nt(stack_heads(q, masks), k) * scale + bias_s[ALL]).astype(BF16)
            outs.append(pick_heads(nn(prob, v), masks))
        att = jnp.concatenate(outs, axis=0)
        gated = (jax.nn.sigmoid(proj[:, 3 * width:]) * att).astype(BF16)
        out = (zc.astype(F32) + nn(gated, w_o[ALL])).astype(BF16)
        z_new[at] = out.reshape(ROWS_STEP, n, -1)
    rows_loop(z.shape[0] // ROWS_STEP, step)


def att_fwd(z, bias, mask, w_qkvg, w_o, heads, cid, extra):
    n = z.shape[1]
    moves = [('gather', bias)] + extra
    return call_with(functools.partial(att_body, heads), moves, [(z.shape, BF16)], [pltpu.VMEM((heads * n, n), F32)],
                     z, mask, w_qkvg, w_o, cid=cid, name='att_fwd', late=tuple(range(1, len(moves))))


def att_back_body(heads, dz, z, bias_g, mask, w_qkvg, w_o, dz_part, d_bias, g_qkvg, g_o, bias_s):
    width = w_o.shape[0]
    n, c = z.shape[1:]
    masks = head_masks(width, heads)
    scale = (width // heads) ** -0.5
    load_bias(bias_g, bias_s, mask[ALL], heads)
    d_bias[ALL] = jnp.zeros_like(d_bias)
    g_qkvg[ALL] = jnp.zeros_like(g_qkvg)
    g_o[ALL] = jnp.zeros_like(g_o)
    step_rows = 2

    def step(t):
        at = pl.ds(t * step_rows, step_rows)
        zc = z[at].reshape(-1, c)
        dzc = dz[at].reshape(-1, c)
        zhat, inv = norm_parts(zc)
        normed = zhat.astype(BF16)
        proj = nn(normed, w_qkvg[ALL])
        qkv = proj[:, :3 * width].astype(BF16)
        gate = jax.nn.sigmoid(proj[:, 3 * width:])
        d_gated = round_bf(nt(dzc, w_o[ALL]))
        d_att = (d_gated * gate).astype(BF16)
        atts, dprojs = [], []
        for s in range(step_rows):
            row = qkv[s * n:(s + 1) * n]
            q, k, v = row[:, :width], row[:, width:2 * width], row[:, 2 * width:]
            qs = stack_heads(q, masks)
            prob = soft(nt(qs, k) * scale + bias_s[ALL])
            prob_b = prob.astype(BF16)
            att = pick_heads(nn(prob_b, v), masks)
            das = stack_heads(d_att[s * n:(s + 1) * n], masks)
            dp = round_bf(nt(das, v))
            ds = prob * (dp - jnp.sum(prob * dp, axis=-1, keepdims=True))
            d_bias[ALL] += ds
            dsb = (ds * scale).astype(BF16)
            dq = pick_heads(nn(dsb, k), masks)
            dk = tn(dsb, qs)
            dv = tn(prob_b, das)
            atts.append(att)
            dprojs.append(jnp.concatenate([dq.astype(BF16), dk.astype(BF16), dv.astype(BF16)], axis=1))
        att = jnp.concatenate(atts, axis=0)
        d_gl = (d_gated * att * gate * (1.0 - gate)).astype(BF16)
        gated = (gate * att).astype(BF16)
        dproj = jnp.concatenate([jnp.concatenate(dprojs, axis=0), d_gl], axis=1)
        g_o[ALL] += tn(gated, dzc)
        g_qkvg[ALL] += tn(normed, dproj)
        dn = round_bf(nt(dproj, w_qkvg[ALL]))
        out = dzc.astype(F32) + norm_back(zhat, inv, dn)
        dz_part[at] = out.reshape(step_rows, n, c)
    rows_loop(z.shape[0] // step_rows, step)


def att_back(dz, z, bias_g, mask, w_qkvg, w_o, heads, cid, turned, extra):
    n = z.shape[1]
    outs = [(z.shape, F32), ((heads * n, n), F32), (w_qkvg.shape, F32), (w_o.shape, F32)]
    body, scratch = functools.partial(att_back_body, heads), [pltpu.VMEM((heads * n, n), F32)]
    moves, args = ([('back', dz)], ()) if turned else ([], (dz,))
    late = tuple(range(len(moves), len(moves) + len(extra)))
    return call_with(body, moves + extra, outs, scratch, *args, z, bias_g, mask, w_qkvg, w_o, cid=cid, name='att_back',
                     late=late)


def bias_back_rows(zc, db, w_t, g_t, t):
    zhat, inv = norm_parts(zc)
    normed = zhat.astype(BF16).reshape(ROWS_STEP, -1, zc.shape[-1])
    dns = []
    for s in range(ROWS_STEP):
        d = db[t * ROWS_STEP + s]
        dns.append(tn(d, w_t[ALL]))
        g_t[ALL] += nn(d, normed[s])
    return norm_back(zhat, inv, round_bf(jnp.concatenate(dns, axis=0)))


def bias_back_body(swap_out, parts, dz_part, z, w_t, dz, g_t, wide, db, *scr):
    g_t[ALL] = jnp.zeros_like(g_t)
    dst = scr[0] if swap_out else dz
    heads = parts.shape[0] // 4
    wide[ALL] = jnp.zeros_like(wide)
    for h in range(heads):
        wide[h] = (parts[h] + parts[heads + h] + parts[2 * heads + h] + parts[3 * heads + h]).astype(BF16)
    swap_lead(wide, db)

    def step(t):
        at = pl.ds(t * ROWS_STEP, ROWS_STEP)
        c = z.shape[-1]
        add = bias_back_rows(z[at].reshape(-1, c), db, w_t, g_t, t)
        dst[at] = (dz_part[at].reshape(-1, c) + add).astype(BF16).reshape(ROWS_STEP, -1, c)
    rows_loop(z.shape[0] // ROWS_STEP, step)
    if swap_out:
        swap_lead(scr[0], dz)


def bias_back(d_bias, dz_part, z, w_t, heads, swap_out, cid):
    r, n, c = z.shape
    out = (n, r, c) if swap_out else (r, n, c)
    scratch = [pltpu.VMEM((16, r, n), BF16), pltpu.VMEM((r, 16, n), BF16)]
    if swap_out:
        scratch.append(pltpu.VMEM((r, n, c), BF16))
    return call_with(functools.partial(bias_back_body, swap_out), [('cols', d_bias.reshape(heads, n, n))],
                     [(out, BF16), (w_t.shape, F32)], scratch, dz_part, z, w_t, cid=cid, name='bias_back')[1]


def turn_body(recv, w_t, z_cols, bias, b1, b2):
    swap_lead(recv, z_cols)

    def step(t):
        zc = z_cols[pl.ds(t * ROWS_STEP, ROWS_STEP)].reshape(-1, z_cols.shape[-1])
        bias_rows(zc, w_t, b1, t)
    rows_loop(z_cols.shape[0] // ROWS_STEP, step)
    swap_lead(b1, b2)
    bias[ALL] = b2[:bias.shape[0]]


def turn(z, w_t, heads, cid):
    r, n, c = z.shape
    scratch = [pltpu.VMEM((r, 16, n), BF16), pltpu.VMEM((16, r, n), BF16)]
    return call_with(turn_body, [('cols', z)], [((r, n, c), BF16), ((heads, r, n), BF16)], scratch, w_t, cid=cid,
                     name='turn')[1]


def pair_trans_body(z, w_up, w_down, w_t, z_new, z_turn, bias):
    inner = w_down.shape[0]

    def step(t):
        at = pl.ds(t * ROWS_STEP, ROWS_STEP)
        zc = z[at].reshape(-1, z.shape[-1])
        normed = norm_parts(zc)[0].astype(BF16)
        hid = nn(normed, w_up[ALL])
        acted = (jax.nn.silu(hid[:, :inner]) * hid[:, inner:]).astype(BF16)
        out = (zc.astype(F32) + nn(acted, w_down[ALL])).astype(BF16)
        z_new[at] = out.reshape(ROWS_STEP, -1, z.shape[-1])
        bias_rows(out, w_t, bias, t)
    rows_loop(z.shape[0] // ROWS_STEP, step)
    swap_lead(z_new, z_turn)


def pair_trans(z, w_up, w_down, w_t):
    r, n, c = z.shape
    return call(pair_trans_body, [((r, n, c), BF16), ((n, r, c), BF16), ((r, 16, n), BF16)], [],
                z, w_up, w_down, w_t, name='pair_trans')


def silu_parts(h1, h2):
    sg = jax.nn.sigmoid(h1)
    return sg, h1 * sg


def pair_trans_back_body(d_recv, z5, db, z, w_up, w_down, w_t, dz_in, g_up, g_down, g_t, dz5):
    inner = w_down.shape[0]
    g_up[ALL] = jnp.zeros_like(g_up)
    g_down[ALL] = jnp.zeros_like(g_down)
    g_t[ALL] = jnp.zeros_like(g_t)
    swap_lead(d_recv, dz5)

    def step(t):
        at = pl.ds(t * ROWS_STEP, ROWS_STEP)
        c = z.shape[-1]
        add = bias_back_rows(z5[at].reshape(-1, c), db, w_t, g_t, t)
        dzc = (dz5[at].reshape(-1, c).astype(F32) + add).astype(BF16)
        zhat, inv = norm_parts(z[at].reshape(-1, c))
        normed = zhat.astype(BF16)
        hid = nn(normed, w_up[ALL])
        h1, h2 = hid[:, :inner], hid[:, inner:]
        sg, si = silu_parts(h1, h2)
        acted = (si * h2).astype(BF16)
        d_act = round_bf(nt(dzc, w_down[ALL]))
        d1 = (d_act * h2 * (sg + si * (1.0 - sg))).astype(BF16)
        d2 = (d_act * si).astype(BF16)
        dh = jnp.concatenate([d1, d2], axis=1)
        g_down[ALL] += tn(acted, dzc)
        g_up[ALL] += tn(normed, dh)
        dn = round_bf(nt(dh, w_up[ALL]))
        out = dzc.astype(F32) + norm_back(zhat, inv, dn)
        dz_in[at] = out.astype(BF16).reshape(ROWS_STEP, -1, c)
    rows_loop(z.shape[0] // ROWS_STEP, step)


def pair_trans_back(d_recv, z5, db, z, w_up, w_down, w_t):
    r, n, c = z.shape
    outs = [((r, n, c), BF16), (w_up.shape, F32), (w_down.shape, F32), (w_t.shape, F32)]
    return call(pair_trans_back_body, outs, [pltpu.VMEM((r, n, c), BF16)], d_recv, z5, db, z, w_up, w_down, w_t,
                name='pair_trans_back')


def put_rows(out, first, blocks, block, value):
    out[pl.ds(first + block, value.shape[0], stride=blocks), :] = value


def single_body(heads, pb_g, s, ds, mask_col, w_qkvg, q_bias, w_o, w_up, w_down, s_new, ds_in, d_pb, grads,
                pb_t, probs, acc_a, acc_b, acc_c, dh_s, act_s):
    c = s.shape[1]
    n = s.shape[0]
    inner = w_down.shape[0]
    size = c // heads
    scale = size ** -0.5
    lane = lax.broadcasted_iota(jnp.int32, (1, c), 1)
    swap_lead(pb_g, pb_t)

    def masked(x, h):
        return jnp.where((lane >= h * size) & (lane < (h + 1) * size), x, jnp.zeros_like(x))

    s_hat, s_inv = norm_parts(s[ALL])
    normed = s_hat.astype(BF16)
    proj = nn(normed, w_qkvg[ALL])
    q = (proj[:, :c] + q_bias[ALL].astype(F32)).astype(BF16)
    k = proj[:, c:2 * c].astype(BF16)
    v = proj[:, 2 * c:3 * c].astype(BF16)
    gate = jax.nn.sigmoid(proj[:, 3 * c:])
    acc_a[ALL] = jnp.zeros_like(acc_a)

    def attend(h):
        logits = nt(k, masked(q, h)) * scale + pb_t[h].astype(F32) + mask_col[ALL]
        e = jnp.exp(logits - jnp.max(logits, axis=0, keepdims=True))
        prob = e / jnp.sum(e, axis=0, keepdims=True)
        probs[h] = prob
        acc_a[ALL] += tn(prob.astype(BF16), masked(v, h))
    rows_loop(heads, attend)
    att = acc_a[ALL]
    gated = (gate * att).astype(BF16)
    s_mid = (s[ALL].astype(F32) + nn(gated, w_o[ALL])).astype(BF16)
    m_hat, m_inv = norm_parts(s_mid)
    mid_n = m_hat.astype(BF16)
    width = c
    dsv = ds[ALL]
    acc_b[ALL] = jnp.zeros_like(acc_b)
    acc_c[ALL] = jnp.zeros_like(acc_c)
    for t in range(inner // width):
        at = slice(t * width, (t + 1) * width)
        at2 = slice(inner + t * width, inner + (t + 1) * width)
        h1 = nn(mid_n, w_up[:, at])
        h2 = nn(mid_n, w_up[:, at2])
        sg, si = silu_parts(h1, h2)
        act = (si * h2).astype(BF16)
        acc_b[ALL] += nn(act, w_down[at, :])
        act_s[:, at] = act
        d_act = round_bf(nt(dsv, w_down[at, :]))
        d1 = (d_act * h2 * (sg + si * (1.0 - sg))).astype(BF16)
        d2 = (d_act * si).astype(BF16)
        dh_s[:, at] = d1
        dh_s[:, at2] = d2
        acc_c[ALL] += nt(d1, w_up[:, at]) + nt(d2, w_up[:, at2])
    s_new[ALL] = (s_mid.astype(F32) + acc_b[ALL]).astype(BF16)
    ds_mid = (dsv.astype(F32) + norm_back(m_hat, m_inv, round_bf(acc_c[ALL]))).astype(BF16)
    rows_qkvg = c * 4 * c // LANES
    off_o = rows_qkvg + c // LANES + pb_t.shape[0]
    off_up = off_o + c * c // LANES
    off_down = off_up + c * 2 * inner // LANES
    cb = c // LANES
    for t in range(2 * inner // c):
        g = tn(mid_n, dh_s[:, t * c:(t + 1) * c])
        for b in range(cb):
            put_rows(grads, off_up, 2 * inner // LANES, t * cb + b, g[:, b * LANES:(b + 1) * LANES])
    for t in range(inner // c):
        g = tn(act_s[:, t * c:(t + 1) * c], dsv)
        for b in range(cb):
            put_rows(grads, off_down + t * c * cb, cb, b, g[:, b * LANES:(b + 1) * LANES])
    g = tn(gated, ds_mid)
    for b in range(cb):
        put_rows(grads, off_o, cb, b, g[:, b * LANES:(b + 1) * LANES])

    d_gated = round_bf(nt(ds_mid, w_o[ALL]))
    d_att = (d_gated * gate).astype(BF16)
    d_gl = (d_gated * att * gate * (1.0 - gate)).astype(BF16)
    acc_a[ALL] = jnp.zeros_like(acc_a)
    acc_b[ALL] = jnp.zeros_like(acc_b)
    acc_c[ALL] = jnp.zeros_like(acc_c)

    def back(h):
        prob = probs[h]
        dam = masked(d_att, h)
        dp = round_bf(nt(v, dam))
        dst = prob * (dp - jnp.sum(prob * dp, axis=0, keepdims=True))
        d_pb[h] = dst.astype(BF16)
        dsb = (dst * scale).astype(BF16)
        acc_a[ALL] += tn(dsb, masked(k, h))
        acc_b[ALL] += nn(dsb, masked(q, h))
        acc_c[ALL] += nn(prob.astype(BF16), dam)
    rows_loop(heads, back)
    parts = [acc_a[ALL].astype(BF16), acc_b[ALL].astype(BF16), acc_c[ALL].astype(BF16), d_gl]
    dn = jnp.zeros((n, c), F32)
    for t in range(4):
        g = tn(normed, parts[t])
        dn = dn + nt(parts[t], w_qkvg[:, t * c:(t + 1) * c])
        for b in range(cb):
            put_rows(grads, 0, 4 * cb, t * cb + b, g[:, b * LANES:(b + 1) * LANES])
    qb = jnp.sum(parts[0].astype(F32), axis=0, keepdims=True)
    for b in range(cb):
        grads[rows_qkvg + b:rows_qkvg + b + 1, :] = qb[:, b * LANES:(b + 1) * LANES]
    grads[rows_qkvg + cb:off_o, :] = jnp.zeros((off_o - rows_qkvg - cb, LANES), F32)
    ds_in[ALL] = (ds_mid.astype(F32) + norm_back(s_hat, s_inv, round_bf(dn))).astype(BF16)


def single_track(s, ds, pbias, extra, mask_col, w_qkvg, q_bias, w_o, w_up, w_down, heads, cid):
    n, c = s.shape
    inner = w_down.shape[0]
    rows = (4 * c * c + c + LANES * heads + c * c + 3 * inner * c) // LANES
    outs = [((n, c), BF16), ((n, c), BF16), ((heads, n, n), BF16), ((rows, LANES), F32)]
    scratch = [pltpu.VMEM((heads, n, n), BF16), pltpu.VMEM((heads, n, n), F32)] + [pltpu.VMEM((n, c), F32)] * 3 + [
        pltpu.VMEM((n, 2 * inner), BF16), pltpu.VMEM((n, inner), BF16)]
    moves = [('rows', pbias)] + extra
    return call_with(functools.partial(single_body, heads), moves, outs, scratch, s, ds, mask_col, w_qkvg, q_bias, w_o,
                     w_up, w_down, cid=cid, name='single_track', late=tuple(range(1, len(moves))))


def pad_bias(w_tb):
    return jnp.pad(w_tb.T, ((0, 16 - w_tb.shape[1]), (0, 0)))


def bias_grad(g_t, heads):
    return g_t[:heads].T.reshape(-1, LANES)


def chunk_rows(total, parts):
    shard = total // parts
    return shard, -(-(shard // LANES + 2) // 32) * 32


def single_pieces(grads, n_pair, total_size):
    group = lax.axis_size(GROUP_AXIS)
    shard, chunk = chunk_rows(total_size, DP_SIZE)
    quarter = chunk // group
    q = lax.axis_index(GROUP_AXIS)
    padded = jnp.pad(grads, ((n_pair, chunk), (0, 0)))
    return jnp.stack([lax.dynamic_slice(padded, (d * shard // LANES + q * quarter, 0), (quarter, LANES))
                      for d in range(DP_SIZE)])


def group_parts(grads):
    rows = flat_rows(grads)
    unit = 8 * DP_SIZE * lax.axis_size(GROUP_AXIS)
    rows = jnp.pad(rows, ((0, -rows.shape[0] % unit), (0, 0)))
    return rows.reshape(lax.axis_size(GROUP_AXIS), -1, LANES)


def owner_parts(landed):
    return jnp.sum(landed, axis=0).reshape(DP_SIZE, -1, LANES)


def finish_grads(own, late, early, n_pair, n_pb, pb_row, total_size):
    parts = lax.axis_size(BATCH_AXIS)
    shard, chunk = chunk_rows(total_size, parts)
    first = lax.axis_index(BATCH_AXIS) * shard // LANES
    n_late = late.shape[0]
    n_early = n_pair - n_late
    pair = jnp.concatenate([late, early[:n_early], jnp.zeros((2 * chunk, LANES), F32)])
    own = own + lax.dynamic_slice(pair, (jnp.minimum(first, n_pair + chunk), 0), (chunk, LANES))
    extra = jnp.pad(early[n_early:n_early + n_pb], ((chunk, chunk), (0, 0)))
    at = jnp.clip(chunk - (pb_row - first), 0, chunk + n_pb)
    own = own + lax.dynamic_slice(extra, (at, 0), (chunk, LANES))
    offset = (lax.axis_index(BATCH_AXIS) * shard) % LANES
    return lax.dynamic_slice(own.reshape(-1), (offset,), (shard,))


def flat_rows(grads):
    return jnp.concatenate([g.reshape(-1, LANES) for g in grads])


def device_step(single_blk, pair_blk, mask_blk, d_single_blk, d_pair_blk, *weights):
    me = lax.axis_index(GROUP_AXIS)
    s_rows, z_zero = single_blk[0], pair_blk[0]
    r = z_zero.shape[0]
    mask = (mask_blk.astype(F32) - 1.0) * MASK_PENALTY
    (mo_in, mo_gate, mo_proj, mi_in, mi_gate, mi_proj, st_qkvg, st_tb, st_o, en_qkvg, en_tb, en_o, p_up, p_down,
     g_qkvg, g_qb, g_pb, g_o, g_up, g_down) = weights
    heads, single_heads = st_tb.shape[1], g_pb.shape[1]
    st_t, en_t, pb_t = pad_bias(st_tb), pad_bias(en_tb), g_pb.T
    total_size = sum(w.size for w in weights)

    left1, right1 = mul_pre(z_zero, mo_in, False)
    (right1_g,), (z_one, xh1, xhat1, rstd1) = mul_post(left1, right1, z_zero, mo_gate, mo_proj, None, heads, False, 0)
    left2, right2, left2_nat = mul_pre(z_one, mi_in, True)
    _, (z_two, xh2, xhat2, rstd2, bias3) = mul_post(left2_nat, right2, z_one, mi_gate, mi_proj, st_t, heads, True, 1)
    half = left1.shape[0] // 2
    (bias3_g, s_all, ds_all, left1_lo), (z_three,) = att_fwd(
        z_two, bias3, mask, st_qkvg, st_o, heads, 2,
        [('rows', s_rows), ('rows', d_single_blk[0]), ('gather', left1[:half])])
    zc_three, bias4 = turn(z_three, en_t, heads, 3)
    (bias4_g, left1_hi), (zc_four,) = att_fwd(zc_three, bias4, mask, en_qkvg, en_o, heads, 4, [('gather', left1[half:])])
    zc_five, z_five_turn, pbias = pair_trans(zc_four, p_up, p_down, pb_t)
    (_, z_five, d_pair_recv), (s_new, ds_in, d_pb, single_grads) = single_track(
        s_all, ds_all, pbias, [('back', z_five_turn), ('cols', d_pair_blk[0])], mask.reshape(-1, 1), g_qkvg,
        g_qb.reshape(1, -1), g_o, g_up, g_down, single_heads, 5)
    n_pair = sum(w.size for w in weights[:14]) // LANES
    pieces = single_pieces(single_grads, n_pair, total_size)
    cut = pieces.shape[1] // 2
    d_pb_own = lax.dynamic_slice_in_dim(d_pb, me * r, r, 1).transpose(1, 0, 2)
    dzc_four, d_pup, d_pdown, d_pbt = pair_trans_back(d_pair_recv, zc_five, d_pb_own, zc_four, p_up, p_down, pb_t)
    (own_lo,), (dz_part4, d_bias4, d_enq, d_eno) = att_back(
        dzc_four, zc_three, bias4_g, mask, en_qkvg, en_o, heads, 12, False, [('dp_parts', pieces[:, :cut])])
    dz_three_turn, d_ent = bias_back(d_bias4, dz_part4, zc_three, en_t, heads, True, 6)
    grads_en = [d_enq, bias_grad(d_ent, heads), d_eno, d_pup, d_pdown, bias_grad(d_pbt, single_heads)]
    (_, own_hi, en_mine), (dz_part3, d_bias3, d_stq, d_sto) = att_back(
        dz_three_turn, z_two, bias3_g, mask, st_qkvg, st_o, heads, 7, True,
        [('dp_parts', pieces[:, cut:]), ('parts', group_parts(grads_en))])
    dz_two, d_stt = bias_back(d_bias3, dz_part3, z_two, st_t, heads, False, 8)
    grads_st = [d_stq, bias_grad(d_stt, heads), d_sto]
    own_single = jnp.concatenate([jnp.sum(own_lo, axis=0), jnp.sum(own_hi, axis=0)])
    (own_all, en_own, st_mine), (dm2, dgp2, d_mip) = mul_back_post(
        dz_two, z_one, xh2, xhat2, rstd2, mi_gate, mi_proj, False, 13,
        [('gather', own_single), ('dp_parts', owner_parts(en_mine)), ('parts', group_parts(grads_st))])
    (_, en_quarter, st_own), (dz_one, d_mii, d_mig) = mul_back_pre(
        [('gather', dm2), ('dp_gather', jnp.sum(en_own, axis=0)), ('dp_parts', owner_parts(st_mine))],
        dz_two, z_one, dgp2, left2, right2, mask, mi_in, mi_gate, True, 9)
    (en_all, st_quarter), (dm1, dgp1, d_mop, dm1_nat) = mul_back_post(
        dz_one, z_zero, xh1, xhat1, rstd1, mo_gate, mo_proj, True, 14,
        [('gather', en_quarter.reshape(-1, LANES)), ('dp_gather', jnp.sum(st_own, axis=0))])
    left1_g = jnp.concatenate([left1_lo, left1_hi], axis=1)
    (_, st_all), (dz_zero, d_moi, d_mog) = mul_back_pre(
        [('cols', dm1_nat), ('gather', st_quarter.reshape(-1, LANES))],
        dz_one, z_zero, dgp1, dm1, right1_g, left1_g, mo_in, mo_gate, False, 10)
    late = total(flat_rows([d_moi, d_mog, d_mop, d_mii, d_mig, d_mip]), 11)
    n_st, n_en = sum(w.size for w in weights[6:9]) // LANES, sum(w.size for w in weights[9:14]) // LANES
    early = jnp.concatenate([st_all.reshape(-1, LANES)[:n_st], en_all.reshape(-1, LANES)[:n_en + single_heads]])
    own_single = own_all.reshape(-1, LANES)
    pb_row = n_pair + (g_qkvg.size + g_qb.size) // LANES
    grad_flat = finish_grads(own_single, late, early, n_pair, single_heads, pb_row, total_size)
    s_out = lax.dynamic_slice_in_dim(s_new, me * r, r, 0)
    ds_out = lax.dynamic_slice_in_dim(ds_in, me * r, r, 0)
    return s_out[None], z_five[None], ds_out[None], dz_zero[None], grad_flat


def solution(mesh):
    spec_single = P(BATCH_AXIS, GROUP_AXIS, None)
    spec_pair = P(BATCH_AXIS, GROUP_AXIS, None, None)
    spec_mask = P(BATCH_AXIS, None)

    def block_fn(single_rep, pair_rep, token_mask, d_single_out, d_pair_out, *weights):
        in_specs = (spec_single, spec_pair, spec_mask, spec_single, spec_pair) + tuple(P() for w_item in weights)
        out_specs = (spec_single, spec_pair, spec_single, spec_pair, P(BATCH_AXIS))
        mapped = jax.shard_map(device_step, mesh=mesh, in_specs=in_specs, out_specs=out_specs, check_vma=False)
        return mapped(single_rep, pair_rep, token_mask, d_single_out, d_pair_out, *weights)

    return block_fn
```

time: 834 us -> 600 us (0.72); the launches traced: 820 us -> 598 us
  waiting for transfers between devices: 375 us -> 0 us
  Pallas kernels: 293 us -> 538 us
  blocking collectives: 55.5 us -> 0 us
  starting transfers between devices: 18.2 us -> 0 us
  local copies, waits for them, and re-layouts: 59.1 us -> 41.1 us
  other arithmetic: 4.87 us -> 18.6 us
  between operations: 14.6 us -> 1.05 us
    pallas_call x0 -> x15, Pallas kernels: none -> 488 us  [the longest x14 454 us: call_with(): pl.pallas_call(whole, out_shape=lands + [jax.ShapeDtypeStruct(sh, d) for...]
    pallas_call x18 -> x4, Pallas kernels: 293 us -> 49.4 us  [call(): pl.pallas_call(body, out_shape=outs, scratch_shapes=scratch, name=name, i...]
    reduce_scatter x3 -> x0, waiting for transfers between devices: 117 us -> none  [the longest x1 76.9 us: reduce_single(): lax.psum_scatter(jnp.concatenate(pieces), BATCH_AXIS, scatter_dimension=0...]
    all_gather x6 -> x0, waiting for transfers between devices: 106 us -> none  [the longest x4 82.8 us: gather(): return lax.all_gather(x, GROUP_AXIS, axis=0, tiled=False)]
    psum x1 -> x0, waiting for transfers between devices: 69.6 us -> none  [finish_grads(): rows = gather_rows(lax.psum(rows, BATCH_AXIS))]
    all_to_all x5 -> x0, waiting for transfers between devices: 54 us -> none  [the longest x4 33 us: exchange(): return lax.all_to_all(x, GROUP_AXIS, 1, 0, tiled=True)]
    all_gather x4 -> x0, blocking collectives: 37.6 us -> none  [gather_rows(): return lax.all_gather(x, GROUP_AXIS, axis=0, tiled=True)]
    unnamed x12 -> x0, waiting for transfers between devices: 28.6 us -> none
  transfers between devices with their start and end apart: 16 -> 0, of which waited for: 13 -> 0; matrix products, arithmetic and copies ran while one was open for 4% -> 0% of each run, Pallas kernels for 8% -> 0%
where the time goes in v2:
time: 600 us; the launch traced here: 598 us
  Pallas kernels  538 us (90%)
  local copies, waits for them, and re-layouts  41.1 us (7%)
  other arithmetic  18.6 us (3%)
    pallas_call x14, Pallas kernels, call_with(): pl.pallas_call(whole, out_shape=lands + [jax.ShapeDtypeStruct(sh, d) for...  454 us
    pallas_call x4, Pallas kernels, call(): pl.pallas_call(body, out_shape=outs, scratch_shapes=scratch, name=name, i...  49.4 us
    pallas_call x1, Pallas kernels, total(): pl.pallas_call(total_body, out_shape=jax.ShapeDtypeStruct(g.shape, F32),...  33.8 us
    unnamed x38, local copies, waits for them, and re-layouts  12.4 us

profile of v2, /device:TPU:0, one launch (start us, length us, event | category | flops | bytes accessed | tf_op | source)
XLA Modules:
  0.0 598.3 jit_solution(8947098912706626520)
XLA Ops:
  0.7 1.3 fusion.10
  1.9 1.2 reshape.77.refs_7_
  3.2 1.3 pad.23.refs_5_.refs_3_
  4.4 1.3 pad.24.refs_1_.refs_3_
  5.8 0.7 copy.32.refs_5_
  6.5 8.7 %mul_pre_out.1 = (bf16[128,32,128]{2,1,0:T(8,128)(2,1)}, bf16[128,32,128]{2,1,0:T(8,128)(2,1)}) custom-call(bf16[32,128,128]{2,1,0:T(8,128)(2,1)} %bitcast.52, bf16[128,512]{1,0:T(8,128)(2,1)} %refs_8_.7), custom_call_target="tpu_custom_call" | custom-call | flops 80000000 | bytes 4000000 | tf_op jit(solution)/shard_map/mul_pre_out/pallas_call | solution.py:79
  15.2 2.3 fusion.12
  17.5 44.7 %mul_post_out.1 = (bf16[4,128,32,128]{3,2,1,0:T(8,128)(2,1)}, bf16[32,128,128]{2,1,0:T(8,128)(2,1)}, bf16[32,128,128]{2,1,0:T(8,128)(2,1)}, f32[128,32,128]{2,1,0:T(8,128)}, f32[32,128]{1,0:T(8,128)}) custom-call(bf16[128,32,128]{2,1,0:T(8,128)(2,1)} %get-tuple-element.79.refs_0_, bf16[128,32,128]{2,1,0:T(8,128)(2,1)} %get-tuple-element.80.refs_1_, ...), custom_call_target="tpu_custom_call" | custom-call | flops 80000000 | bytes 4000000 | tf_op jit(solution)/shard_map/mul_post_out/pallas_call | solution.py:206
  62.1 9.0 %mul_pre_in.1 = (bf16[128,32,128]{2,1,0:T(8,128)(2,1)}, bf16[128,32,128]{2,1,0:T(8,128)(2,1)}, bf16[32,128,128]{2,1,0:T(8,128)(2,1)}) custom-call(bf16[32,128,128]{2,1,0:T(8,128)(2,1)} %get-tuple-element.81.z.refs_2_.refs_4_, bf16[128,512]{1,0:T(8,128)(2,1)} %refs_9_.6), custom_call_target="tpu_custom_call" | custom-call | flops 80000000 | bytes 4000000 | tf_op jit(solution)/shard_map/mul_pre_in/pallas_call | solution.py:79
  71.2 58.1 %mul_post_in.1 = (bf16[128,32,128]{2,1,0:T(8,128)(2,1)}, bf16[4,128,32,128]{3,2,1,0:T(8,128)(2,1)}, bf16[32,128,128]{2,1,0:T(8,128)(2,1)}, bf16[32,128,128]{2,1,...) custom-call(bf16[32,128,128]{2,1,0:T(8,128)(2,1)} %get-tuple-element.82.refs_0_, ...), custom_call_target="tpu_custom_call" | custom-call | flops 80000000 | bytes 4000000 | tf_op jit(solution)/shard_map/mul_post_in/pallas_call | solution.py:206
  129.3 22.5 %att_fwd.2 = (bf16[4,4,32,128]{3,2,1,0:T(8,128)(2,1)}, bf16[128,384]{1,0:T(8,128)(2,1)}, bf16[128,384]{1,0:T(8,128)(2,1)}, bf16[4,64,32,128]{3,2,1,0:T(8,128)(2,1)}, bf16[32,128,128]{2,1,0:T(8,128)(2,1)}) custom-call(bf16[4,32,128]{2,1,0:T(8,128)(2,1)} %get-tuple-element.84.refs_0_, bf16[32,384]{1,0:T(8,128)(2,1)} %bitcast.70, bf16[32,384]{1,0:T(8,128)(2,1)} %bitcast.71, ...), custom_call_target="tpu_custom_call" | custom-call | flops 80000000 | bytes 4000000 | tf_op jit(solution)/shard_map/att_fwd/pallas_call | solution.py:206
  151.8 20.2 %turn.1 = (bf16[128,32,128]{2,1,0:T(8,128)(2,1)}, bf16[32,128,128]{2,1,0:T(8,128)(2,1)}, bf16[4,32,128]{2,1,0:T(8,128)(2,1)}) custom-call(bf16[32,128,128]{2,1,0:T(8,128)(2,1)} %get-tuple-element.86.refs_0_, bf16[16,128]{1,0:T(8,128)(2,1)} %pad.24.refs_1_.refs_3_), custom_call_target="tpu_custom_call" | custom-call | flops 80000000 | bytes 4000000 | tf_op jit(solution)/shard_map/turn/pallas_call | solution.py:206
  172.0 21.2 %att_fwd.3 = (bf16[4,4,32,128]{3,2,1,0:T(8,128)(2,1)}, bf16[4,64,32,128]{3,2,1,0:T(8,128)(2,1)}, bf16[32,128,128]{2,1,0:T(8,128)(2,1)}) custom-call(bf16[4,32,128]{2,1,0:T(8,128)(2,1)} %get-tuple-element.87.refs_0_, bf16[64,32,128]{2,1,0:T(8,128)(2,1)} %get-tuple-element.155.refs_1_, bf16[32,128,128]{2,1,0:T(8,128)(2,1)} %get-tuple-element.88.refs_2_, ...), custom_call_target="tpu_custom_call" | custom-call | flops 80000000 | bytes 4000000 | tf_op jit(solution)/shard_map/att_fwd/pallas_call | solution.py:206
  193.2 3.9 pad_maximum_fusion.refs_7_
  197.1 12.3 %pair_trans.1 = (bf16[32,128,128]{2,1,0:T(8,128)(2,1)}, bf16[128,32,128]{2,1,0:T(8,128)(2,1)}, bf16[32,16,128]{2,1,0:T(8,128)(2,1)}) custom-call(bf16[32,128,128]{2,1,0:T(8,128)(2,1)} %get-tuple-element.89.z, bf16[128,1024]{1,0:T(8,128)(2,1)} %w_up.3, bf16[512,128]{1,0:T(8,128)(2,1)} %w_down.3, bf16[16,128]{1,0:T(8,128)(2,1)} %bitcast.72), custom_call_target="tpu_custom_call" | custom-call | flops 80000000 | bytes 4000000 | tf_op jit(solution)/shard_map/pair_trans/pallas_call | solution.py:79
  209.4 39.7 %single_track.1 = (bf16[128,16,128]{2,1,0:T(8,128)(2,1)}, bf16[32,128,128]{2,1,0:T(8,128)(2,1)}, bf16[128,32,128]{2,1,0:T(8,128)(2,1)}, bf16[128,384]{1,0:T(8,12...) custom-call(bf16[32,16,128]{2,1,0:T(8,128)(2,1)} %get-tuple-element.90.refs_0_, ...), custom_call_target="tpu_custom_call" | custom-call | flops 80000000 | bytes 4000000 | tf_op jit(solution)/shard_map/single_track/pallas_call | solution.py:206
  249.1 1.4 dynamic-slice_bitcast_fusion.1
  250.4 1.4 copy.33
  251.8 0.7 dynamic-slice_bitcast_fusion.db
  252.5 19.4 %pair_trans_back.1 = (bf16[32,128,128]{2,1,0:T(8,128)(2,1)}, f32[128,1024]{1,0:T(8,128)}, f32[512,128]{1,0:T(8,128)}, f32[16,128]{1,0:T(8,128)}) custom-call(bf16[128,32,128]{2,1,0:T(8,128)(2,1)} %get-tuple-element.98.d_recv, bf16[32,128,128]{2,1,0:T(8,128)(2,1)} %get-tuple-element.99.z5, bf16[32,16,128]{2,1,0:T(8,128)(2,1)} %dynamic-slice_bitcast_fusion.db, ...), custom_call_target="tpu_custom_call" | custom-call | flops 80000000 | bytes 4000000 | tf_op jit(solution)/shard_map/pair_trans_back/pallas_call | solution.py:79
  271.9 0.8 copy.35
  272.8 1.1 reshape.81
  273.9 0.2 bitcast_dynamic-update-slice_fusion.7
  274.1 3.6 copy-done
  278.0 0.2 bitcast_dynamic-update-slice_fusion.5
  278.6 0.2 bitcast_dynamic-update-slice_fusion.2
  279.3 1.9 fusion.11
  281.2 44.3 %att_back.2 = (f32[8,376,128]{2,1,0:T(8,128)}, f32[32,128,128]{2,1,0:T(8,128)}, f32[512,128]{1,0:T(8,128)}, f32[128,512]{1,0:T(8,128)}, f32[128,128]{1,0:T(8,128)}) custom-call(f32[8,376,128]{2,1,0:T(8,128)} %get-tuple-element.154.refs_0_, bf16[32,128,128]{2,1,0:T(8,128)(2,1)} %get-tuple-element.101.refs_1_, ...), custom_call_target="tpu_custom_call" | custom-call | flops 80000000 | bytes 4000000 | tf_op jit(solution)/shard_map/att_back/pallas_call | solution.py:206
  325.5 1.5 reduce_sum.54
  327.0 13.2 %bias_back.2 = (f32[16,32,128]{2,1,0:T(8,128)}, bf16[128,32,128]{2,1,0:T(8,128)(2,1)}, f32[16,128]{1,0:T(8,128)}) custom-call(f32[4,128,128]{2,1,0:T(8,128)} %bitcast.68, f32[32,128,128]{2,1,0:T(8,128)} %get-tuple-element.105.refs_1_, bf16[32,128,128]{2,1,0:T(8,128)(2,1)} %get-tuple-element.88.refs_2_, bf16[16,128]{1,0:T(8,128)(2,1)} %pad.24.refs_1_.refs_3_), custom_call_target="tpu_custom_call" | custom-call | flops 80000000 | bytes 4000000 | tf_op jit(solution)/shard_map/bias_back/pallas_call | solution.py:206
  340.2 0.7 slice_bitcast_fusion.1
  341.2 1.5 concatenate.21
  342.7 1.1 pad.26
  343.8 54.1 %att_back.3 = (bf16[32,128,128]{2,1,0:T(8,128)(2,1)}, f32[8,376,128]{2,1,0:T(8,128)}, f32[4,576,128]{2,1,0:T(8,128)}, f32[32,128,128]{2,1,0:T(8,128)}, f32[512,1...) custom-call(bf16[128,32,128]{2,1,0:T(8,128)(2,1)} %get-tuple-element.106.refs_0_, ...), custom_call_target="tpu_custom_call" | custom-call | flops 80000000 | bytes 4000000 | tf_op jit(solution)/shard_map/att_back/pallas_call | solution.py:206
  398.0 1.5 reduce_sum.55
  399.5 0.8 pad_maximum_fusion.1.refs_0_
  400.3 1.0 reshape.85
  401.3 12.5 %bias_back.3 = (f32[16,32,128]{2,1,0:T(8,128)}, bf16[32,128,128]{2,1,0:T(8,128)(2,1)}, f32[16,128]{1,0:T(8,128)}) custom-call(f32[4,128,128]{2,1,0:T(8,128)} %bitcast.67, f32[32,128,128]{2,1,0:T(8,128)} %get-tuple-element.118.refs_1_, bf16[32,128,128]{2,1,0:T(8,128)(2,1)} %get-tuple-element.85.refs_4_.refs_3_.refs_2_, bf16[16,128]{1,0:T(8,128)(2,1)} %pad.23.refs_5_.refs_3_), custom_call_target="tpu_custom_call" | custom-call | flops 80000000 | bytes 4000000 | tf_op jit(solution)/shard_map/bias_back/pallas_call | solution.py:206
  413.7 0.7 slice_bitcast_fusion
  414.6 0.8 select_maximum_fusion
  415.4 0.8 reduce_sum.56
  416.2 22.8 %mul_back_post.2 = (f32[4,752,128]{2,1,0:T(8,128)}, f32[8,72,128]{2,1,0:T(8,128)}, f32[4,192,128]{2,1,0:T(8,128)}, bf16[128,32,128]{2,1,0:T(8,128)(2,1)}, bf16[3...) custom-call(f32[752,128]{1,0:T(8,128)} %pad_maximum_fusion.1.refs_0_, f32[8,72,128]{2,1,0:T(8,128)} %bitcast.58, ...), custom_call_target="tpu_custom_call" | custom-call | flops 80000000 | bytes 4000000 | tf_op jit(solution)/shard_map/mul_back_post/pallas_call | solution.py:206
  439.1 1.6 reduce_sum.57.refs_1_
  440.7 1.7 reduce_sum.58
  442.3 47.5 %mul_back_pre_in.1 = (bf16[4,128,32,128]{3,2,1,0:T(8,128)(2,1)}, f32[8,72,128]{2,1,0:T(8,128)}, f32[8,24,128]{2,1,0:T(8,128)}, bf16[32,128,128]{2,1,0:T(8,128)(2...) custom-call(bf16[128,32,128]{2,1,0:T(8,128)(2,1)} %get-tuple-element.125.refs_0_, f32[72,128]{1,0:T(8,128)} %reduce_sum.57.refs_1_, ...), custom_call_target="tpu_custom_call" | custom-call | flops 80000000 | bytes 4000000 | tf_op jit(solution)/shard_map/mul_back_pre_in/pallas_call | solution.py:206
  489.9 1.5 reduce_sum.59.refs_1_
  491.4 1.7 reshape.94
  493.0 16.7 %mul_back_post.3 = (f32[4,576,128]{2,1,0:T(8,128)}, f32[8,24,128]{2,1,0:T(8,128)}, bf16[128,32,128]{2,1,0:T(8,128)(2,1)}, bf16[32,128,128]{2,1,0:T(8,128)(2,1)},...) custom-call(f32[576,128]{1,0:T(8,128)} %bitcast.65, f32[24,128]{1,0:T(8,128)} %reduce_sum.59.refs_1_, ...), custom_call_target="tpu_custom_call" | custom-call | flops 80000000 | bytes 4000000 | tf_op jit(solution)/shard_map/mul_back_post/pallas_call | solution.py:206
  509.8 36.9 %mul_back_pre_out.1 = (bf16[128,32,128]{2,1,0:T(8,128)(2,1)}, f32[4,192,128]{2,1,0:T(8,128)}, bf16[32,128,128]{2,1,0:T(8,128)(2,1)}, f32[128,512]{1,0:T(8,128)}, f32[128,128]{1,0:T(8,128)}) custom-call(bf16[32,128,128]{2,1,0:T(8,128)(2,1)} %get-tuple-element.136.refs_0_, f32[192,128]{1,0:T(8,128)} %bitcast.69, ...), custom_call_target="tpu_custom_call" | custom-call | flops 80000000 | bytes 4000000 | tf_op jit(solution)/shard_map/mul_back_pre_out/pallas_call | solution.py:206
  546.7 0.7 slice.45
  547.4 1.4 slice.44
  548.8 1.7 reshape.93
  550.5 1.7 slice.43
  552.2 1.0 constant_dynamic-update-slice_fusion.5
  553.2 0.8 constant_dynamic-update-slice_fusion.4
  554.1 0.8 constant_dynamic-update-slice_fusion.3
  554.9 1.0 constant_dynamic-update-slice_fusion.2
  555.9 0.8 constant_dynamic-update-slice_fusion.1
  556.7 0.9 copy-done.3
  557.6 33.8 %total.1 = f32[1536,128]{1,0:T(8,128)} custom-call(f32[1536,128]{1,0:T(8,128)} %copy-done.3), custom_call_target="tpu_custom_call" | custom-call | flops 80000000 | bytes 4000000 | tf_op jit(solution)/shard_map/total/pallas_call | solution.py:271
  591.5 3.2 fusion.1
  594.7 1.6 dynamic_slice.55
  596.3 1.0 copy.51
  597.3 1.0 copy.52
  (36 shorter events, 1.7 us)
Async XLA Ops:
  151.8 41.4 %copy-start.1 = (bf16[4,64,32,128]{3,2,1,0:T(8,128)(2,1)S(1)}, bf16[4,64,32,128]{3,2,1,0:T(8,128)(2,1)}, u32[]{:S(2)}) copy-start(bf16[4,64,32,128]{3,2,1,0:T(8,128)(2,1)} %get-tuple-element.141) | copy-start | bytes 6291460
  273.9 3.9 copy-start
  325.5 15.7 %copy-start.8 = (f32[128,512]{1,0:T(8,128)S(1)}, f32[128,512]{1,0:T(8,128)}, u32[]{:S(2)}) copy-start(f32[128,512]{1,0:T(8,128)} %get-tuple-element.107) | copy-start | bytes 786436
  325.5 15.7 %copy-start.7 = (f32[512,128]{1,0:T(8,128)S(1)}, f32[512,128]{1,0:T(8,128)}, u32[]{:S(2)}) copy-start(f32[512,128]{1,0:T(8,128)} %get-tuple-element.111) | copy-start | bytes 786436
  325.5 15.7 %copy-start.9 = (f32[128,128]{1,0:T(8,128)S(1)}, f32[128,128]{1,0:T(8,128)}, u32[]{:S(2)}) copy-start(f32[128,128]{1,0:T(8,128)} %get-tuple-element.109) | copy-start | bytes 196612
  398.0 16.7 %copy-start.11 = (f32[128,128]{1,0:T(8,128)S(1)}, f32[128,128]{1,0:T(8,128)}, u32[]{:S(2)}) copy-start(f32[128,128]{1,0:T(8,128)} %get-tuple-element.120) | copy-start | bytes 196612
  399.5 15.9 %copy-start.4 = (f32[4,576,128]{2,1,0:T(8,128)S(1)}, f32[4,576,128]{2,1,0:T(8,128)}, u32[]{:S(2)}) copy-start(f32[4,576,128]{2,1,0:T(8,128)} %get-tuple-element.115) | copy-start | bytes 3538948
  546.6 10.1 %copy-start.10 = (f32[128,128]{1,0:T(8,128)S(1)}, f32[128,128]{1,0:T(8,128)}, u32[]{:S(2)}) copy-start(f32[128,128]{1,0:T(8,128)} %get-tuple-element.150) | copy-start | bytes 196612
  547.4 44.1 %copy-start.2 = (f32[4,752,128]{2,1,0:T(8,128)S(1)}, f32[4,752,128]{2,1,0:T(8,128)}, u32[]{:S(2)}) copy-start(f32[4,752,128]{2,1,0:T(8,128)} %get-tuple-element.144) | copy-start | bytes 4620292
  556.7 0.9 copy-start.3
  591.5 4.8 copy-start.5
  594.7 2.6 copy-start.6
